TPU v7x, 256 devices: a whole 4x4x8 slice. The times are simulated.
256 devices in a mesh: agent: 32 (over x, y, core), res: 8 (over z).
Axes of the slice: x: 4, y: 4, z: 8, core: 2. Of those that a mesh axis runs over, the one named last changes fastest.
Arguments:
- linear_cost: float32 [8192, 2048], P('agent', 'res'), may hold values from -6 to 6
- agent_type: int32 [8192], P('agent'), may hold values from 0 to 3, as said below
- block_mask: int32 [8192, 16], P('agent', 'res'), may hold values 0 or 1
- inverses: bfloat16 [4, 2048, 2048], P(None, 'res'), as said below
- cost_weight: float32 [2048], P('res'), may hold values from 0.5 to 8
- target: float32 [2048], P('res'), may hold values from -6 to 6
Outputs:
- usage: float32 [8192, 2048], P('agent', 'res')
- shared: float32 [2048], P('res')
- prices: float32 [2048], P('res')
- primal_norm: float32 [5], replicated
- dual_norm: float32 [5], replicated
Inputs may be any that keep to these rules, and one draw needn't show every extreme that they name: Each inverses[k] is exactly symmetric: inverses[k, i, j] equals inverses[k, j, i]. `agent_type`: each aligned block of 256 agents (the agents held by one device along the agent axis) holds exactly 64 agents of each type, in no particular order.
All inputs are finite; a program needn't handle non-finite values. No bound on the sum of `block_mask` on one device may be relied on, other than what follows from the above.
Results may differ from a plain program's by a relative error of at most 0.0039.
Values may be sent and summed in bfloat16 or wider, within the bound.
A program may use at most 64 MiB of HBM per device.

v0:
```python
import jax
import jax.numpy as jnp
from jax import lax
from jax.sharding import PartitionSpec as P

BLK = 128
ITERS = 5


penalty = 1.0
eps = 1e-06


def laid_out(blocks, dim):
    blocks = jnp.moveaxis(blocks, 0, dim)
    dims = blocks.shape
    return blocks.reshape(*dims[:dim], dims[dim] * dims[dim + 1], *dims[dim + 2 :])


def sent_to_all(x, axis):
    size = lax.axis_size(axis)
    return lax.all_to_all(jnp.broadcast_to(x[None], (size, *x.shape)), axis, 0, 0, tiled=True)


def gathered_copies(x, axis, dim):
    return laid_out(sent_to_all(x, axis), dim)


def of_everyone(x, axis):
    return sent_to_all(x, axis).sum(axis=0)


def in_one(arrays, axis):
    ends = [0]
    for a in arrays:
        ends.append(ends[-1] + a.size)
    so_far = of_everyone(jnp.concatenate([a.ravel() for a in arrays]), axis)
    return tuple((so_far[b:e].reshape(a.shape) for a, b, e in zip(arrays, ends, ends[1:])))


def on_device(linear_cost, agent_type, block_mask, inverses, cost_weight, target):
    local_agents, local_width = linear_cost.shape
    type_count = inverses.shape[0]
    group_rows = local_agents // type_count
    count = local_agents * lax.axis_size("agent")
    block_count = block_mask.shape[1]
    order = jnp.argsort(agent_type, stable=True)
    restore = jnp.argsort(order, stable=True)
    expand = jnp.broadcast_to(
        block_mask.astype(jnp.float32)[:, :, None], (local_agents, block_count, BLK)
    ).reshape(local_agents, local_width)
    usage = jnp.zeros(linear_cost.shape, jnp.float32)
    mean_usage = jnp.zeros((local_width,), jnp.float32)
    shared = jnp.zeros((local_width,), jnp.float32)
    prices = jnp.zeros((local_width,), jnp.float32)
    gap_list = []
    change_list = []
    for iteration in range(ITERS):
        rhs = (penalty * (usage - mean_usage + shared - prices) - linear_cost).astype(jnp.bfloat16)
        grouped = rhs[order].reshape(type_count, group_rows, local_width)
        product = jnp.einsum(
            "tas,tws->taw",
            gathered_copies(grouped, "res", 2),
            inverses,
            preferred_element_type=jnp.float32,
        )
        new_usage = product.reshape(local_agents, local_width)[restore]
        new_usage = new_usage * expand
        change_local = penalty * penalty * jnp.sum((new_usage - usage) ** 2)
        usage = new_usage
        column_sum = jnp.sum(usage, axis=0)
        usage_sum, change_agents = in_one((column_sum, change_local), "agent")
        mean_usage = usage_sum / count
        shared = (cost_weight * target + penalty * (prices + mean_usage)) / (cost_weight + penalty)
        prices = prices + mean_usage - shared
        gap_list.append(count * jnp.sum((mean_usage - shared) ** 2))
        change_list.append(change_agents)
    gap_totals, change_totals = in_one((jnp.stack(gap_list), jnp.stack(change_list)), "res")
    primal_norm = jnp.sqrt(gap_totals + eps)
    dual_norm = jnp.sqrt(change_totals + eps)
    return (usage, shared, prices, primal_norm, dual_norm)


def solution(mesh):
    placed = (
        P("agent", "res"),
        P("agent"),
        P("agent", "res"),
        P(None, "res", None),
        P("res"),
        P("res"),
    )
    return jax.shard_map(
        on_device,
        mesh=mesh,
        in_specs=placed,
        out_specs=(P("agent", "res"), P("res"), P("res"), P(), P()),
        check_vma=False,
    )
```

profile of v0, /device:TPU:32, one launch (start us, length us, event | category | flops | bytes accessed | tf_op | source)
XLA Modules:
  0.0 278.4 jit_solution(11882291761102320020)
XLA Ops:
  0.7 3.8 %sort.31 = (s32[256]{0:T(256)}, s32[256]{0:T(256)S(1)}) sort(s32[256]{0:T(256)} %param.7, s32[256]{0:T(256)S(1)} %iota.7), dimensions={0}, to_apply=%region_0.0 | sort | flops 2048 | bytes 4096 | tf_op jit(solution)/shard_map/jit(argsort)/sort | solution.py:47
  4.5 1.0 subtract_convert_fusion.4
  5.5 1.2 gather_fusion
  6.6 1.1 broadcast_in_dim.43
  7.7 8.6 %all-to-all-start = ((bf16[8,4,64,256]{3,2,1,0:T(8,128)(2,1)}), bf16[8,4,64,256]{3,2,1,0:T(8,128)(2,1)S(1)}, u32[]{:S(2)}, u32[]{:S(2)}) async-start(bf16[8,4,64,256]{3,2,1,0:T(8,128)(2,1)} %broadcast_in_dim.43), calls=%async_computation | async-start | bytes 2097152 | tf_op jit(solution)/shard_map/all_to_all | solution.py:22
  16.3 3.2 %sort.32 = (s32[256]{0:T(256)}, s32[256]{0:T(256)S(1)}) sort(s32[256]{0:T(256)S(1)} %get-tuple-element.7, s32[256]{0:T(256)S(1)} %iota.8), dimensions={0}, to_apply=%region_1.2 | sort | flops 2048 | bytes 4096 | tf_op jit(solution)/shard_map/jit(argsort)/sort | solution.py:48
  19.5 0.1 copy.25
  19.7 23.9 %all-to-all-done = bf16[8,4,64,256]{3,2,1,0:T(8,128)(2,1)S(1)} async-done(((bf16[8,4,64,256]{3,2,1,0:T(8,128)(2,1)}), bf16[8,4,64,256]{3,2,1,0:T(8,128)(2,1)S(1)}, u32[]{:S(2)}, u32[]{:S(2)}) %all-to-all-start) | async-done | bytes 1048608 | tf_op jit(solution)/shard_map/all_to_all | solution.py:22
  43.6 0.1 copy.51
  43.7 3.6 %fusion.15 = f32[4,64,256]{2,1,0:T(8,128)S(1)} fusion(bf16[4,64,2048]{2,1,0:T(8,128)(2,1)S(1)} %bitcast.73, bf16[4,256,2048]{2,1,0:T(8,128)(2,1)} %param.9), kind=kOutput, calls=%fused_computation.66 | convolution fusion | flops 268435456 | bytes 5505024 | tf_op jit(solution)/shard_map/tas,tws->taw/dot_general | solution.py:61
  47.4 1.0 gather_fusion.1
  48.4 0.3 broadcast_in_dim.45
  48.7 0.7 fusion.13
  49.4 0.7 pad_maximum_fusion
  50.1 14.6 %all_to_all.61 = f32[32,1,257]{2,1,0:T(1,128)S(1)} all-to-all(f32[32,1,257]{2,1,0:T(1,128)S(1)} %broadcast_in_dim.46), channel_id=1, replica_groups=mesh['agent'=32,'res'=8] {'agent'}, dimensions={0} | all-to-all | bytes 65792 | tf_op jit(solution)/shard_map/all_to_all | solution.py:22
  64.7 0.6 multiply_reduce_fusion.9
  65.4 1.2 gather_fusion.2
  66.7 32.0 %all_to_all.62 = bf16[8,4,64,256]{3,2,1,0:T(8,128)(2,1)S(1)} all-to-all(bf16[8,4,64,256]{3,2,1,0:T(8,128)(2,1)S(1)} %broadcast_in_dim.48), channel_id=1, replica_groups=mesh['agent'=32,'res'=8] {'res'}, dimensions={0} | all-to-all | bytes 2097152 | tf_op jit(solution)/shard_map/all_to_all | solution.py:22
  98.7 0.1 copy.52
  98.8 1.4 fusion.16
  100.2 1.0 gather_fusion.3
  101.2 0.7 fusion.12
  101.8 0.7 pad_maximum_fusion.1
  102.5 10.7 %all_to_all.63 = f32[32,1,257]{2,1,0:T(1,128)S(1)} all-to-all(f32[32,1,257]{2,1,0:T(1,128)S(1)} %broadcast_in_dim.49), channel_id=1, replica_groups=mesh['agent'=32,'res'=8] {'agent'}, dimensions={0} | all-to-all | bytes 65792 | tf_op jit(solution)/shard_map/all_to_all | solution.py:22
  113.3 0.6 multiply_reduce_fusion.8
  114.0 1.2 gather_fusion.4
  115.3 32.0 %all_to_all.64 = bf16[8,4,64,256]{3,2,1,0:T(8,128)(2,1)S(1)} all-to-all(bf16[8,4,64,256]{3,2,1,0:T(8,128)(2,1)S(1)} %broadcast_in_dim.51), channel_id=1, replica_groups=mesh['agent'=32,'res'=8] {'res'}, dimensions={0} | all-to-all | bytes 2097152 | tf_op jit(solution)/shard_map/all_to_all | solution.py:22
  147.3 0.1 copy.53
  147.4 1.4 fusion.17
  148.8 1.0 gather_fusion.5
  149.8 0.7 fusion.11
  150.5 0.7 pad_maximum_fusion.2
  151.1 10.7 %all_to_all.65 = f32[32,1,257]{2,1,0:T(1,128)S(1)} all-to-all(f32[32,1,257]{2,1,0:T(1,128)S(1)} %broadcast_in_dim.52), channel_id=1, replica_groups=mesh['agent'=32,'res'=8] {'agent'}, dimensions={0} | all-to-all | bytes 65792 | tf_op jit(solution)/shard_map/all_to_all | solution.py:22
  161.9 0.6 multiply_reduce_fusion.7
  162.6 1.2 gather_fusion.6
  163.9 32.0 %all_to_all.66 = bf16[8,4,64,256]{3,2,1,0:T(8,128)(2,1)S(1)} all-to-all(bf16[8,4,64,256]{3,2,1,0:T(8,128)(2,1)S(1)} %broadcast_in_dim.54), channel_id=1, replica_groups=mesh['agent'=32,'res'=8] {'res'}, dimensions={0} | all-to-all | bytes 2097152 | tf_op jit(solution)/shard_map/all_to_all | solution.py:22
  195.9 0.1 copy.54
  196.0 1.4 fusion.18
  197.4 1.0 gather_fusion.7
  198.4 0.7 fusion.10
  199.1 0.7 pad_maximum_fusion.3
  199.7 10.7 %all_to_all.67 = f32[32,1,257]{2,1,0:T(1,128)S(1)} all-to-all(f32[32,1,257]{2,1,0:T(1,128)S(1)} %broadcast_in_dim.55), channel_id=1, replica_groups=mesh['agent'=32,'res'=8] {'agent'}, dimensions={0} | all-to-all | bytes 65792 | tf_op jit(solution)/shard_map/all_to_all | solution.py:22
  210.5 0.6 multiply_reduce_fusion.6
  211.2 1.2 gather_fusion.8
  212.5 32.0 %all_to_all.68 = bf16[8,4,64,256]{3,2,1,0:T(8,128)(2,1)S(1)} all-to-all(bf16[8,4,64,256]{3,2,1,0:T(8,128)(2,1)S(1)} %broadcast_in_dim.57), channel_id=1, replica_groups=mesh['agent'=32,'res'=8] {'res'}, dimensions={0} | all-to-all | bytes 2097152 | tf_op jit(solution)/shard_map/all_to_all | solution.py:22
  244.6 1.4 fusion.19
  246.0 1.0 gather_fusion.9
  247.0 1.4 fusion.9
  248.4 0.7 pad_maximum_fusion.4
  249.1 0.6 broadcast_in_dim.58
  249.7 3.9 %all-to-all-start.9 = ((f32[32,1,257]{2,1,0:T(1,128)}), f32[32,1,257]{2,1,0:T(1,128)S(1)}, u32[]{:S(2)}, u32[]{:S(2)}) async-start(f32[32,1,257]{2,1,0:T(1,128)} %broadcast_in_dim.58), calls=%async_computation.9 | async-start | bytes 98304 | tf_op jit(solution)/shard_map/all_to_all | solution.py:22
  253.6 0.5 slice.41
  254.8 0.5 slice.42
  255.9 0.6 slice.43
  257.2 0.5 slice.44
  258.3 2.7 all-to-all-done.9
  261.1 0.6 slice.45
  261.7 0.6 multiply_reduce_fusion.5
  263.0 3.2 %concatenate.23 = f32[10]{0:T(128)S(1)} concatenate(f32[1]{0:T(128)} %bitcast.20, f32[1]{0:T(128)} %bitcast.21, f32[1]{0:T(128)} %bitcast.22, f32[1]{0:T(128)} %bitcast.23, f32[1]{0:T(128)} %bitcast.24, f32[1]{0:T(128)} %slice.41, f32[1]{0:T(128)} %slice.42, f32[1]{0:T(128)} %slice.43, f32[1]{0:T(128)} %slice.44, f32[1]{0:T(128)} %slice.45), dimensions={0} | concatenate | bytes 80 | tf_op jit(solution)/shard_map/concatenate | solution.py:37
  266.2 0.6 broadcast_in_dim.59
  266.8 4.7 %all-to-all-start.10 = ((f32[8,1,10]{2,1,0:T(1,128)}), f32[8,1,10]{2,1,0:T(1,128)S(1)}, u32[]{:S(2)}, u32[]{:S(2)}) async-start(f32[8,1,10]{2,1,0:T(1,128)} %broadcast_in_dim.59), calls=%async_computation.10 | async-start | bytes 8192 | tf_op jit(solution)/shard_map/all_to_all | solution.py:22
  271.5 0.6 fusion.1
  272.1 5.7 %all-to-all-done.10 = f32[8,1,10]{2,1,0:T(1,128)S(1)} async-done(((f32[8,1,10]{2,1,0:T(1,128)}), f32[8,1,10]{2,1,0:T(1,128)S(1)}, u32[]{:S(2)}, u32[]{:S(2)}) %all-to-all-start.10) | async-done | bytes 352 | tf_op jit(solution)/shard_map/all_to_all | solution.py:22
  277.8 0.6 add_sqrt_fusion
  (47 shorter events, 1.3 us)
Async XLA Ops:
  0.6 18.9 %copy-start.7 = (s32[256,2]{0,1:T(2,128)S(1)}, s32[256,2]{0,1:T(2,128)}, u32[]{:S(2)}) copy-start(s32[256,2]{0,1:T(2,128)} %param.8) | copy-start | bytes 6148
  7.7 35.8 %all-to-all-start = ((bf16[8,4,64,256]{3,2,1,0:T(8,128)(2,1)}), bf16[8,4,64,256]{3,2,1,0:T(8,128)(2,1)S(1)}, u32[]{:S(2)}, u32[]{:S(2)}) async-start(bf16[8,4,64,256]{3,2,1,0:T(8,128)(2,1)} %broadcast_in_dim.43), calls=%async_computation | async-start | bytes 2097152 | tf_op jit(solution)/shard_map/all_to_all | solution.py:22
  43.7 21.0 %copy-start.5 = (f32[256]{0:T(256)S(1)}, f32[256]{0:T(256)}, u32[]{:S(2)}) copy-start(f32[256]{0:T(256)} %param.10) | copy-start | bytes 3076
  43.7 21.0 %copy-start.8 = (f32[256]{0:T(256)S(1)}, f32[256]{0:T(256)}, u32[]{:S(2)}) copy-start(f32[256]{0:T(256)} %param.11) | copy-start | bytes 3076
  43.7 21.6 %copy-start.4 = (f32[256,256]{1,0:T(8,128)S(1)}, f32[256,256]{1,0:T(8,128)}, u32[]{:S(2)}) copy-start(f32[256,256]{1,0:T(8,128)} %param.6) | copy-start | bytes 786436
  66.6 32.2 %copy-start = (bf16[4,256,2048]{2,1,0:T(8,128)(2,1)S(1)}, bf16[4,256,2048]{2,1,0:T(8,128)(2,1)}, u32[]{:S(2)}) copy-start(bf16[4,256,2048]{2,1,0:T(8,128)(2,1)} %param.9) | copy-start | bytes 12582916
  115.2 32.2 %copy-start.1 = (bf16[4,256,2048]{2,1,0:T(8,128)(2,1)S(1)}, bf16[4,256,2048]{2,1,0:T(8,128)(2,1)}, u32[]{:S(2)}) copy-start(bf16[4,256,2048]{2,1,0:T(8,128)(2,1)} %param.9) | copy-start | bytes 12582916
  163.8 32.2 %copy-start.2 = (bf16[4,256,2048]{2,1,0:T(8,128)(2,1)S(1)}, bf16[4,256,2048]{2,1,0:T(8,128)(2,1)}, u32[]{:S(2)}) copy-start(bf16[4,256,2048]{2,1,0:T(8,128)(2,1)} %param.9) | copy-start | bytes 12582916
  212.4 32.2 %copy-start.3 = (bf16[4,256,2048]{2,1,0:T(8,128)(2,1)S(1)}, bf16[4,256,2048]{2,1,0:T(8,128)(2,1)}, u32[]{:S(2)}) copy-start(bf16[4,256,2048]{2,1,0:T(8,128)(2,1)} %param.9) | copy-start | bytes 12582916
  249.7 11.3 %all-to-all-start.9 = ((f32[32,1,257]{2,1,0:T(1,128)}), f32[32,1,257]{2,1,0:T(1,128)S(1)}, u32[]{:S(2)}, u32[]{:S(2)}) async-start(f32[32,1,257]{2,1,0:T(1,128)} %broadcast_in_dim.58), calls=%async_computation.9 | async-start | bytes 98304 | tf_op jit(solution)/shard_map/all_to_all | solution.py:22
  262.4 16.0 %copy-start.6 = (f32[256]{0:T(256)}, f32[256]{0:T(256)S(1)}, u32[]{:S(2)}) copy-start(f32[256]{0:T(256)S(1)} %get-tuple-element.20) | copy-start | bytes 3076
  266.8 11.0 %all-to-all-start.10 = ((f32[8,1,10]{2,1,0:T(1,128)}), f32[8,1,10]{2,1,0:T(1,128)S(1)}, u32[]{:S(2)}, u32[]{:S(2)}) async-start(f32[8,1,10]{2,1,0:T(1,128)} %broadcast_in_dim.59), calls=%async_computation.10 | async-start | bytes 8192 | tf_op jit(solution)/shard_map/all_to_all | solution.py:22
where the time goes:
time: 280 us; the launch traced here: 278 us
  blocking collectives  175 us (62%)
  waiting for transfers between devices  32.4 us (12%)
  local copies, waits for them, and re-layouts  20.6 us (7%)
  other arithmetic  20.2 us (7%)
  starting transfers between devices  17.1 us (6%)
  matrix products  9.21 us (3%)
  between operations  4.24 us (2%)
    all_to_all x8, blocking collectives, sent_to_all(): lax.all_to_all(jnp.broadcast_to(x[None], (size, *x.shape)), axis, 0, 0, t...  175 us
    all_to_all x3, waiting for transfers between devices, sent_to_all(): lax.all_to_all(jnp.broadcast_to(x[None], (size, *x.shape)), axis, 0, 0, t...  32.4 us
    all_to_all x3, starting transfers between devices, sent_to_all(): lax.all_to_all(jnp.broadcast_to(x[None], (size, *x.shape)), axis, 0, 0, t...  17.1 us
    dot_general x5, matrix products, on_device(): jnp.einsum('tas,tws->taw', gathered_copies(grouped, 'res', 2), inverses,...  9.21 us
    gather x5, local copies, waits for them, and re-layouts, on_device(): grouped = rhs[order].reshape(type_count, group_rows, local_width)  5.76 us
  transfers between devices with their start and end apart: 3, of which 3 were waited for; matrix products, arithmetic and copies ran while one was open for 2% of the time, Pallas kernels for 0%

commit v1 on v0

v1 whole, which is shorter than its diff:
```python
import functools

import jax
import jax.numpy as jnp
from jax import lax
from jax.experimental import pallas as pl
from jax.experimental.pallas import tpu as pltpu
from jax.sharding import PartitionSpec as P

ITERS = 5
AGENTS = 8192
EPS = 1e-06
MESH = pl.DeviceIdType.MESH
F32 = jnp.float32
BF16 = jnp.bfloat16


def three_parts(value):
    high = value.astype(BF16).astype(F32)
    rest = value - high
    mid = rest.astype(BF16).astype(F32)
    return high, mid, rest - mid


def kernel(
    cost_ref, type_ref, mask_ref, weight_ref, target_ref, inv_ref,
    usage_out, shared_out, prices_out, primal_out, dual_out,
    mats, order, packed, rows, expand, usage, rhs, vectors, plane, lines, back,
    mat_load, z_send, z_recv, one_send, one_recv, two_send, two_recv, core_send, core_recv,
    row_send, row_recv, plane_send, plane_recv, line_send, line_recv, back_send, back_recv,
):
    agent, z = lax.axis_index("agent"), lax.axis_index("res")
    x, y, c = agent // 8, (agent // 2) % 4, agent % 2
    kind = z % 4
    first, second = x * (1 - c) + y * c, y * (1 - c) + x * c
    place = x * 4 + y

    def at(px, py, pc, pz):
        return (px * 8 + py * 2 + pc, pz)

    def along(step_one, step_two):
        one, two = (first + step_one) % 4, (second + step_two) % 4
        return at(one * (1 - c) + two * c, two * (1 - c) + one * c, c, z)

    def copy(src, dst, send, recv, device):
        return pltpu.make_async_remote_copy(src, dst, send, recv, device_id=device, device_id_type=MESH)

    def plane_peer(e):
        other = (place + e) % 16
        return at(other // 4, other % 4, c, z)

    def line_peer(e):
        other = (c * 8 + z + e) % 16
        return other // 8, other % 8

    barrier = pltpu.get_barrier_semaphore()

    def greet(e, carry):
        pl.semaphore_signal(barrier, inc=1, device_id=plane_peer(e), device_id_type=MESH)
        pc, pz = line_peer(e)
        pl.semaphore_signal(barrier, inc=1, device_id=at(x, y, pc, pz), device_id_type=MESH)
        return carry

    lax.fori_loop(1, 16, greet, 0)
    own_loads = [
        pltpu.make_async_copy(
            inv_ref.at[kind, pl.ds(q * 16, 16), pl.ds(h * 1024, 1024)],
            mats.at[h, z, q // 4, q % 4],
            mat_load.at[h * 16 + q],
        )
        for h in range(2)
        for q in range(16)
    ]
    for load in own_loads:
        load.start()
    pl.semaphore_wait(barrier, 30)

    def z_copy(d):
        far = (z + d) % 8
        return copy(
            inv_ref.at[far % 4, pl.ds((first * 4 + second) * 16, 16), pl.ds(pl.multiple_of(c * 1024, 1024), 1024)],
            mats.at[c, z, first, second],
            z_send.at[d],
            z_recv.at[d],
            at(x, y, c, far),
        )

    for d in (4, 3, 5, 2, 6, 1, 7):
        z_copy(d).start()

    kinds = type_ref[...]
    is_kind = (lax.broadcasted_iota(jnp.int32, (16, 256), 0) == kinds).astype(F32)
    before = (
        lax.broadcasted_iota(jnp.int32, (256, 256), 0) < lax.broadcasted_iota(jnp.int32, (256, 256), 1)
    ).astype(BF16)
    ahead = jnp.dot(is_kind.astype(BF16), before, preferred_element_type=F32)
    spot = kinds * 64 + jnp.sum(is_kind * ahead, axis=0, keepdims=True).astype(jnp.int32)
    order[...] = (lax.broadcasted_iota(jnp.int32, (256, 256), 0) == spot).astype(F32).astype(BF16)
    cost = jnp.dot(order[...], cost_ref[...].astype(BF16), preferred_element_type=F32).astype(BF16)
    extra = jnp.concatenate(
        [mask_ref[...].astype(F32), jnp.zeros((14, 256), F32)], axis=0
    ).astype(BF16)
    masks = lax.dot_general(extra, order[...], (((1,), (1,)), ((), ())), preferred_element_type=F32)
    line = lax.broadcasted_iota(jnp.int32, (16, 256), 0)
    lane = lax.broadcasted_iota(jnp.int32, (16, 256), 1)
    tail = jnp.zeros((16, 256), F32)
    for r, part in enumerate(three_parts(weight_ref[...]) + three_parts(target_ref[...])):
        tail = jnp.where(line == 2 + r, part, tail)
    for t in range(4):
        packed[t, :64] = cost[t * 64 : (t + 1) * 64]
        turned = masks if t == 0 else pltpu.roll(masks, 256 - 64 * t, 1)
        packed[t, 64:] = jnp.where((line < 2) & (lane < 64), turned, tail).astype(BF16)

    def row_copy(e):
        pc, pz = line_peer(e)
        return copy(
            packed.at[pz % 4], rows.at[z, c], row_send.at[e], row_recv.at[e], at(x, y, pc, pz)
        )

    def start_rows(e, carry):
        row_copy(e).start()
        return carry

    lax.fori_loop(1, 16, start_rows, 0)
    rows[z, c] = packed[kind]

    def part(d):
        return mats.at[c, (z - d + 8) % 8]

    def one_copy(d, s):
        block = part(d).at[first, second]
        return copy(block, block, one_send.at[d, s], one_recv.at[d, s], along(s, 0))

    def two_copy(d, s):
        block = part(d).at[:, second]
        return copy(block, block, two_send.at[d, s], two_recv.at[d, s], along(0, s))

    def core_copy(d):
        return copy(part(d), part(d), core_send.at[d], core_recv.at[d], at(x, y, 1 - c, z))

    for d in (1, 7, 2, 6, 3, 5, 4):
        z_copy(d).wait_recv()
        for s in (2, 1, 3):
            one_copy(d, s).start()
    for d in (1, 7, 2, 6, 3, 5, 4):
        for s in (2, 1, 3):
            one_copy(d, s).wait_recv()
        for s in (2, 1, 3):
            two_copy(d, s).start()

    def wait_rows(e, carry):
        row_copy(e).wait_recv()
        return carry

    lax.fori_loop(1, 16, wait_rows, 0)
    wide = (lax.broadcasted_iota(jnp.int32, (16, 256), 1) // 128 == line).astype(F32).astype(BF16)
    for j in range(8):
        ends = rows[j, 0, 64:].astype(F32)
        vectors[0, j : j + 1] = ends[2:3] + ends[3:4] + ends[4:5]
        vectors[1, j : j + 1] = ends[5:6] + ends[6:7] + ends[7:8]
        for half in range(2):
            here = rows[j, half, 64:, :128]
            spread = lax.dot_general(here, wide, (((0,), (0,)), ((), ())), preferred_element_type=F32)
            expand[j, half * 64 : half * 64 + 64] = spread[:64]

    usage[...] = jnp.zeros_like(usage)
    for v in (2, 3, 4):
        vectors[v] = jnp.zeros((8, 256), F32)

    for d in (1, 7, 2, 6, 3, 5, 4):
        for s in (2, 1, 3):
            two_copy(d, s).wait_recv()
        core_copy(d).start()
    for load in own_loads:
        load.wait()
    for d in (1, 7, 2, 6, 3, 5, 4):
        core_copy(d).wait_recv()

    norm_lane = lax.broadcasted_iota(jnp.int32, (1, 128), 1)

    def back_copy(e):
        far = (z + e) % 8
        return copy(
            usage.at[far, pl.ds(pl.multiple_of(c * 64, 64), 64)],
            back.at[kind],
            back_send.at[e],
            back_recv.at[e],
            at(x, y, c, far),
        )

    def iteration(it, norms):
        primal_norms, dual_norms = norms
        par = it

        def right_side(j, carry):
            shift = vectors[3, pl.ds(j, 1)] - vectors[2, pl.ds(j, 1)] - vectors[4, pl.ds(j, 1)]
            costs = rows[j, :, :64].astype(F32).reshape(128, 256)
            rhs[:, pl.ds(pl.multiple_of(j * 256, 256), 256)] = (usage[j] + shift - costs).astype(BF16)
            return carry

        lax.fori_loop(0, 8, right_side, 0)

        def product(j, change):
            block = mats[j // 4, :, :, :, :, pl.ds(pl.multiple_of((j % 4) * 256, 256), 256)].reshape(2048, 256)
            fresh = jnp.dot(rhs[...], block, preferred_element_type=F32) * expand[j]
            gap = fresh - usage[j]
            usage[j] = fresh
            plane[par, place, pl.ds(j, 1)] = jnp.sum(fresh, axis=0, keepdims=True)
            return change + jnp.sum(gap * gap, axis=0, keepdims=True)

        change = lax.fori_loop(0, 8, product, jnp.zeros((1, 256), F32))
        plane[par, place, 8:] = jnp.broadcast_to(change, (8, 256))

        def plane_copy(e):
            return copy(
                plane.at[par, place], plane.at[par, place], plane_send.at[e], plane_recv.at[par, e], plane_peer(e)
            )

        def start_plane(e, carry):
            plane_copy(e).start()
            return carry

        def end_plane(e, carry):
            plane_copy(e).wait()
            return carry

        lax.fori_loop(1, 16, start_plane, 0)
        lax.fori_loop(1, 16, end_plane, 0)
        lines[par, kind] = jnp.sum(plane[par], axis=0)

        def line_copy(e):
            return copy(
                lines.at[par, kind], lines.at[par, kind], line_send.at[e], line_recv.at[par, e],
                at(x, y, c, (z + (1, 7, 2)[e]) % 8),
            )

        for e in range(3):
            line_copy(e).start()
        for e in range(3):
            line_copy(e).wait()
        total = jnp.sum(lines[par], axis=0)
        mean = total[:8] * (1.0 / AGENTS)
        prices = vectors[4]
        shared = (vectors[0] * vectors[1] + (prices + mean)) / (vectors[0] + 1.0)
        vectors[2] = mean
        vectors[3] = shared
        vectors[4] = prices + mean - shared
        gap = mean - shared
        primal = float(AGENTS) * jnp.sum(gap * gap)
        dual = jnp.sum(total[8:9])
        return (
            jnp.where(norm_lane == it, primal, primal_norms),
            jnp.where(norm_lane == it, dual, dual_norms),
        )

    zero = jnp.zeros((1, 128), F32)
    primal_norms, dual_norms = lax.fori_loop(0, ITERS, iteration, (zero, zero))
    for e in (1, 7, 2):
        back_copy(e).start()
    back[kind] = usage[z, pl.ds(pl.multiple_of(c * 64, 64), 64)]
    primal_out[...] = jnp.sqrt(primal_norms + EPS)
    dual_out[...] = jnp.sqrt(dual_norms + EPS)
    shared_out[...] = vectors[3, pl.ds(z, 1)]
    prices_out[...] = vectors[4, pl.ds(z, 1)]
    for e in (1, 7, 2):
        back_copy(e).wait_recv()
    result = jnp.zeros((256, 256), F32)
    for piece in three_parts(back[...].reshape(256, 256)):
        result += lax.dot_general(
            order[...], piece.astype(BF16), (((0,), (0,)), ((), ())), preferred_element_type=F32
        )
    usage_out[...] = result

    def end_rows(e, carry):
        row_copy(e).wait_send()
        return carry

    lax.fori_loop(1, 16, end_rows, 0)
    for d in range(1, 8):
        z_copy(d).wait_send()
        for s in (1, 2, 3):
            one_copy(d, s).wait_send()
            two_copy(d, s).wait_send()
        core_copy(d).wait_send()
    for e in (1, 7, 2):
        back_copy(e).wait_send()


def on_device(linear_cost, agent_type, block_mask, inverses, cost_weight, target):
    vmem = pl.BlockSpec(memory_space=pltpu.VMEM)
    dma = pltpu.SemaphoreType.DMA
    usage, shared, prices, primal, dual = pl.pallas_call(
        kernel,
        out_shape=(
            jax.ShapeDtypeStruct((256, 256), F32),
            jax.ShapeDtypeStruct((1, 256), F32),
            jax.ShapeDtypeStruct((1, 256), F32),
            jax.ShapeDtypeStruct((1, 128), F32),
            jax.ShapeDtypeStruct((1, 128), F32),
        ),
        in_specs=[vmem] * 5 + [pl.BlockSpec(memory_space=pl.ANY)],
        out_specs=(vmem,) * 5,
        scratch_shapes=[
            pltpu.VMEM((2, 8, 4, 4, 16, 1024), BF16),
            pltpu.VMEM((256, 256), BF16),
            pltpu.VMEM((4, 80, 256), BF16),
            pltpu.VMEM((8, 2, 80, 256), BF16),
            pltpu.VMEM((8, 128, 256), F32),
            pltpu.VMEM((8, 128, 256), F32),
            pltpu.VMEM((128, 2048), BF16),
            pltpu.VMEM((5, 8, 256), F32),
            pltpu.VMEM((ITERS, 16, 16, 256), F32),
            pltpu.VMEM((ITERS, 4, 16, 256), F32),
            pltpu.VMEM((4, 64, 256), F32),
            dma((32,)),
            dma((8,)), dma((8,)),
            dma((8, 4)), dma((8, 4)),
            dma((8, 4)), dma((8, 4)),
            dma((8,)), dma((8,)),
            dma((16,)), dma((16,)),
            dma((16,)), dma((ITERS, 16)),
            dma((3,)), dma((ITERS, 3)),
            dma((8,)), dma((8,)),
        ],
        compiler_params=pltpu.CompilerParams(
            collective_id=0, has_side_effects=True, vmem_limit_bytes=60 * 2**20
        ),
        name="admm",
    )(
        linear_cost,
        agent_type.reshape(1, -1),
        block_mask.T,
        cost_weight.reshape(1, -1),
        target.reshape(1, -1),
        inverses,
    )
    return usage, shared.reshape(-1), prices.reshape(-1), primal[0, :ITERS], dual[0, :ITERS]


def solution(mesh):
    placed = (
        P("agent", "res"),
        P("agent"),
        P("agent", "res"),
        P(None, "res", None),
        P("res"),
        P("res"),
    )
    return jax.shard_map(
        on_device,
        mesh=mesh,
        in_specs=placed,
        out_specs=(P("agent", "res"), P("res"), P("res"), P(), P()),
        check_vma=False,
    )
```

time: 280 us -> 127 us (0.45)
  blocking collectives: 175 us -> 0 us
  Pallas kernels: 0 us -> 121 us
  waiting for transfers between devices: 32.4 us -> 0 us
  other arithmetic: 20.2 us -> 0 us
  starting transfers between devices: 17.1 us -> 0 us
  local copies, waits for them, and re-layouts: 20.6 us -> 5.33 us
  matrix products: 9.21 us -> 0 us
  between operations: 4.24 us -> 0.64 us
    all_to_all x8 -> x0, blocking collectives: 175 us -> none  [sent_to_all(): lax.all_to_all(jnp.broadcast_to(x[None], (size, *x.shape)), axis, 0, 0, t...]
    pallas_call x0 -> x1, Pallas kernels: none -> 121 us  [on_device(): pl.pallas_call(kernel, out_shape=(jax.ShapeDtypeStruct((256, 256), F32),...]
    all_to_all x3 -> x0, waiting for transfers between devices: 32.4 us -> none  [sent_to_all(): lax.all_to_all(jnp.broadcast_to(x[None], (size, *x.shape)), axis, 0, 0, t...]
    all_to_all x3 -> x0, starting transfers between devices: 17.1 us -> none  [sent_to_all(): lax.all_to_all(jnp.broadcast_to(x[None], (size, *x.shape)), axis, 0, 0, t...]
    gather x10 -> x0, local copies, waits for them, and re-layouts: 10.6 us -> none  [the longest x5 5.76 us: on_device(): grouped = rhs[order].reshape(type_count, group_rows, local_width)]
    dot_general x5 -> x0, matrix products: 9.21 us -> none  [on_device(): jnp.einsum('tas,tws->taw', gathered_copies(grouped, 'res', 2), inverses,...]
    reduce_sum x16 -> x0, other arithmetic: 7.52 us -> none  [the longest x5 4.14 us: on_device(): column_sum = jnp.sum(usage, axis=0)]
    sort x2 -> x0, other arithmetic: 7.01 us -> none  [the longest x1 3.84 us: on_device(): order = jnp.argsort(agent_type, stable=True)]
  transfers between devices with their start and end apart: 3 -> 0, of which waited for: 3 -> 0; matrix products, arithmetic and copies ran while one was open for 2% -> 0% of each run, Pallas kernels for 0% -> 0%
where the time goes in v1:
time: 127 us
  Pallas kernels  121 us (95%)
  local copies, waits for them, and re-layouts  5.33 us (4%)
    pallas_call x1, Pallas kernels, on_device(): pl.pallas_call(kernel, out_shape=(jax.ShapeDtypeStruct((256, 256), F32),...  121 us
    unnamed x3, local copies, waits for them, and re-layouts  4.13 us

profile of v1, /device:TPU:32, one launch (start us, length us, event | category | flops | bytes accessed | tf_op | source)
XLA Modules:
  0.0 126.6 jit_solution(2373714946580077010)
XLA Ops:
  0.6 120.6 %admm.1 = (f32[256,256]{1,0:T(8,128)}, f32[1,256]{1,0:T(1,128)}, f32[1,256]{1,0:T(1,128)}, f32[1,128]{1,0:T(1,128)}, f32[1,128]{1,0:T(1,128)}) custom-call(f32[256,256]{1,0:T(8,128)} %cost_ref.1, s32[1,256]{1,0:T(1,128)} %bitcast.13, s32[2,256]{1,0:T(2,128)} %bitcast.10, f32[1,256]{1,0:T(1,128)} %bitcast.14, f32[1,256]{1,0:T(1,128)} %bitcast.15, ...), custom_call_target="tpu_custom_call" | custom-call | tf_op jit(solution)/shard_map/admm/pallas_call | solution.py:292
  121.3 1.2 slice_bitcast_fusion
  122.5 1.7 %copy.14 = f32[256,256]{1,0:T(8,128)} copy(f32[256,256]{1,0:T(8,128)} %get-tuple-element.22) | data formatting | bytes 524288
  124.1 1.2 copy.15
  125.3 1.2 copy.16

commit v2 on v1

v2 whole, which is shorter than its diff:
```python
import functools

import jax
import jax.numpy as jnp
from jax import lax
from jax.experimental import pallas as pl
from jax.experimental.pallas import tpu as pltpu
from jax.sharding import PartitionSpec as P

ITERS = 5
AGENTS = 8192
EPS = 1e-06
MESH = pl.DeviceIdType.MESH
F32 = jnp.float32
BF16 = jnp.bfloat16


def three_parts(value):
    high = value.astype(BF16).astype(F32)
    rest = value - high
    mid = rest.astype(BF16).astype(F32)
    return high, mid, rest - mid


def kernel(
    cost_ref, type_ref, mask_ref, weight_ref, target_ref, inv_ref,
    usage_out, small_out,
    mats, order, packed, rows, expand, usage, others, rhs, shift, vectors, plane, lines, back,
    mat_load, z_send, z_recv, one_send, one_recv, two_send, two_recv, core_send, core_recv,
    row_send, row_recv, hand_send, hand_recv, plane_send, plane_recv, line_send, line_recv, back_send, back_recv,
):
    agent, z = lax.axis_index("agent"), lax.axis_index("res")
    x, y, c = agent // 8, (agent // 2) % 4, agent % 2
    kind = z % 4
    first, second = x * (1 - c) + y * c, y * (1 - c) + x * c
    place = x * 4 + y

    def at(px, py, pc, pz):
        return (px * 8 + py * 2 + pc, pz)

    def along(step_one, step_two):
        one, two = (first + step_one) % 4, (second + step_two) % 4
        return at(one * (1 - c) + two * c, two * (1 - c) + one * c, c, z)

    def copy(src, dst, send, recv, device):
        return pltpu.make_async_remote_copy(src, dst, send, recv, device_id=device, device_id_type=MESH)

    def plane_peer(e):
        other = (place + e) % 16
        return at(other // 4, other % 4, c, z)

    barrier = pltpu.get_barrier_semaphore()

    def greet(e, carry):
        pl.semaphore_signal(barrier, inc=1, device_id=plane_peer(e), device_id_type=MESH)
        return carry

    lax.fori_loop(1, 16, greet, 0)
    for d in range(1, 8):
        pl.semaphore_signal(barrier, inc=1, device_id=at(x, y, c, (z + d) % 8), device_id_type=MESH)
    pl.semaphore_signal(barrier, inc=1, device_id=at(x, y, 1 - c, z), device_id_type=MESH)
    own_loads = [
        pltpu.make_async_copy(
            inv_ref.at[kind, pl.ds(q * 16, 16), pl.ds(h * 1024, 1024)],
            mats.at[h, z, q // 4, q % 4],
            mat_load.at[h * 16 + q],
        )
        for h in range(2)
        for q in range(16)
    ]
    for load in own_loads:
        load.start()
    pl.semaphore_wait(barrier, 23)

    def z_copy(d):
        far = (z + d) % 8
        return copy(
            inv_ref.at[far % 4, pl.ds((first * 4 + second) * 16, 16), pl.ds(pl.multiple_of(c * 1024, 1024), 1024)],
            mats.at[c, z, first, second],
            z_send.at[d],
            z_recv.at[d],
            at(x, y, c, far),
        )

    for d in (4, 3, 5, 2, 6, 1, 7):
        z_copy(d).start()

    kinds = type_ref[...]
    is_kind = (lax.broadcasted_iota(jnp.int32, (16, 256), 0) == kinds).astype(F32)
    before = (
        lax.broadcasted_iota(jnp.int32, (256, 256), 0) < lax.broadcasted_iota(jnp.int32, (256, 256), 1)
    ).astype(BF16)
    ahead = jnp.dot(is_kind.astype(BF16), before, preferred_element_type=F32)
    spot = kinds * 64 + jnp.sum(is_kind * ahead, axis=0, keepdims=True).astype(jnp.int32)
    order[...] = (lax.broadcasted_iota(jnp.int32, (256, 256), 0) == spot).astype(F32).astype(BF16)
    cost = jnp.dot(order[...], cost_ref[...].astype(BF16), preferred_element_type=F32).astype(BF16)
    extra = jnp.concatenate(
        [mask_ref[...].astype(F32), jnp.zeros((14, 256), F32)], axis=0
    ).astype(BF16)
    masks = lax.dot_general(extra, order[...], (((1,), (1,)), ((), ())), preferred_element_type=F32)
    line = lax.broadcasted_iota(jnp.int32, (16, 256), 0)
    lane = lax.broadcasted_iota(jnp.int32, (16, 256), 1)
    tail = jnp.zeros((16, 256), F32)
    for r, part in enumerate(three_parts(weight_ref[...]) + three_parts(target_ref[...])):
        tail = jnp.where(line == 2 + r, part, tail)
    for t in range(4):
        packed[t, :64] = cost[t * 64 : (t + 1) * 64]
        turned = masks if t == 0 else pltpu.roll(masks, 256 - 64 * t, 1)
        packed[t, 64:] = jnp.where((line < 2) & (lane < 64), turned, tail).astype(BF16)

    def row_copy(d):
        far = (z + d) % 8
        return copy(packed.at[far % 4], rows.at[z, c], row_send.at[d], row_recv.at[d], at(x, y, c, far))

    def hand_copy(d):
        block = rows.at[(z - d + 8) % 8, c]
        return copy(block, block, hand_send.at[d], hand_recv.at[d], at(x, y, 1 - c, z))

    for d in (4, 3, 5, 2, 6, 1, 7):
        row_copy(d).start()
    rows[z, c] = packed[kind]
    hand_copy(0).start()

    def part(d):
        return mats.at[c, (z - d + 8) % 8]

    def one_copy(d, s):
        block = part(d).at[first, second]
        return copy(block, block, one_send.at[d, s], one_recv.at[d, s], along(s, 0))

    def two_copy(d, s):
        block = part(d).at[:, second]
        return copy(block, block, two_send.at[d, s], two_recv.at[d, s], along(0, s))

    def core_copy(d):
        return copy(part(d), part(d), core_send.at[d], core_recv.at[d], at(x, y, 1 - c, z))

    for d in (1, 7, 2, 6, 3, 5, 4):
        z_copy(d).wait_recv()
        for s in (2, 1, 3):
            one_copy(d, s).start()
    for d in (1, 7, 2, 6, 3, 5, 4):
        for s in (2, 1, 3):
            one_copy(d, s).wait_recv()
        for s in (2, 1, 3):
            two_copy(d, s).start()
    for d in (1, 7, 2, 6, 3, 5, 4):
        row_copy(d).wait_recv()
        hand_copy(d).start()

    for d in range(8):
        hand_copy(d).wait_recv()
    wide = (lax.broadcasted_iota(jnp.int32, (16, 256), 1) // 128 == line).astype(F32).astype(BF16)
    for j in range(8):
        ends = rows[j, 0, 64:].astype(F32)
        vectors[0, j : j + 1] = ends[2:3] + ends[3:4] + ends[4:5]
        vectors[1, j : j + 1] = ends[5:6] + ends[6:7] + ends[7:8]
        for half in range(2):
            here = rows[j, half, 64:, :128]
            spread = lax.dot_general(here, wide, (((0,), (0,)), ((), ())), preferred_element_type=F32)
            expand[j, half * 64 : half * 64 + 64] = spread[:64]

    for d in (1, 7, 2, 6, 3, 5, 4):
        for s in (2, 1, 3):
            two_copy(d, s).wait_recv()
        core_copy(d).start()
    for load in own_loads:
        load.wait()
    for d in (1, 7, 2, 6, 3, 5, 4):
        core_copy(d).wait_recv()

    norm_lane = lax.broadcasted_iota(jnp.int32, (1, 128), 1)

    def back_copy(e):
        far = (z + e) % 8
        return copy(
            usage.at[far, pl.ds(pl.multiple_of(c * 64, 64), 64)],
            back.at[kind],
            back_send.at[e],
            back_recv.at[e],
            at(x, y, c, far),
        )

    def place_columns(k, j, value):
        plane[k, place, pl.ds(j, 1)] = jnp.sum(value, axis=0, keepdims=True)

    def plane_copy(k, tall, e):
        block = plane.at[k, place, pl.ds(0, tall)]
        return copy(block, block, plane_send.at[k, e], plane_recv.at[k, e], plane_peer(e))

    def start_plane(k, tall):
        def start(e, carry):
            plane_copy(k, tall, e).start()
            return carry

        lax.fori_loop(1, 16, start, 0)

    def end_plane(k, tall):
        def end(e, carry):
            plane_copy(k, tall, e).wait_recv()
            return carry

        lax.fori_loop(1, 16, end, 0)
        return jnp.sum(plane[k, :, :tall], axis=0)

    def line_copy(k, tall, e):
        block = lines.at[k, kind, pl.ds(0, tall)]
        return copy(block, block, line_send.at[k, e], line_recv.at[k, e], at(x, y, c, (z + (1, 7, 2)[e]) % 8))

    def start_line(k, value):
        tall = value.shape[0]
        lines[k, kind, :tall] = value
        for e in range(3):
            line_copy(k, tall, e).start()

    def end_line(k, tall):
        for e in range(3):
            line_copy(k, tall, e).wait_recv()
        return jnp.sum(lines[k, :, :tall], axis=0)

    def block_of(j):
        return mats[j // 4, :, :, :, :, pl.ds(pl.multiple_of((j % 4) * 256, 256), 256)].reshape(2048, 256)

    def lanes_of(j):
        return pl.ds(pl.multiple_of(j * 256, 256), 256)

    def costs_of(j):
        return rows[j, :, :64].astype(F32).reshape(128, 256)

    def product(j):
        return jnp.dot(rhs[...], block_of(j), preferred_element_type=F32)

    def applied(k, summed=True):
        def step(j, carry):
            fresh = product(j)
            others[j] = fresh
            if summed:
                place_columns(k, j, fresh * expand[j])
            return carry

        lax.fori_loop(0, 8, step, 0)

    def common(v):
        high, mid, low = three_parts(v)
        for j in range(8):
            stack = jnp.where(line == 0, high[j : j + 1], jnp.where(line == 1, mid[j : j + 1], low[j : j + 1]))
            shift[:, j * 256 : (j + 1) * 256] = jnp.where(line < 3, stack, 0.0).astype(BF16)

        def step(j, carry):
            out = jnp.dot(shift[...], block_of(j), preferred_element_type=F32)
            vectors[4, pl.ds(j, 1)] = out[0:1] + out[1:2] + out[2:3]
            return carry

        lax.fori_loop(0, 8, step, 0)
        return vectors[4]

    def advance(k, last=False):
        def step(j, change):
            fresh = (others[j] + vectors[4, pl.ds(j, 1)]) * expand[j]
            gap = fresh - usage[j]
            usage[j] = fresh
            if last:
                place_columns(4, j, fresh)
            else:
                rhs[:, lanes_of(j)] = (fresh - costs_of(j)).astype(BF16)
            return change + jnp.sum(gap * gap, axis=0, keepdims=True)

        change = lax.fori_loop(0, 8, step, jnp.zeros((1, 256), F32))
        plane[4, place, 7 + k : 8 + k] = change

    def settle(total, prices, norms, k):
        mean = total * (1.0 / AGENTS)
        shared = (vectors[0] * vectors[1] + (prices + mean)) / (vectors[0] + 1.0)
        prices = prices + mean - shared
        gap = mean - shared
        norms = jnp.where(norm_lane == k - 1, float(AGENTS) * jnp.sum(gap * gap), norms)
        return shared - mean - prices, shared, prices, norms

    def negated(j, carry):
        rhs[:, lanes_of(j)] = -rows[j, :, :64].reshape(128, 256)
        return carry

    lax.fori_loop(0, 8, negated, 0)

    def opening(j, change):
        fresh = product(j) * expand[j]
        usage[j] = fresh
        place_columns(0, j, fresh)
        return change + jnp.sum(fresh * fresh, axis=0, keepdims=True)

    change = lax.fori_loop(0, 8, opening, jnp.zeros((1, 256), F32))
    plane[4, place, 8:9] = change
    for j in range(8):
        plane[0, place, 8 + j : 9 + j] = jnp.sum(expand[j], axis=0, keepdims=True)
    start_plane(0, 16)

    def second_side(j, carry):
        rhs[:, lanes_of(j)] = (usage[j] - costs_of(j)).astype(BF16)
        return carry

    lax.fori_loop(0, 8, second_side, 0)
    applied(1)
    start_plane(1, 8)
    sums = end_plane(0, 16)
    start_line(0, sums[:8])
    counts = sums[8:]
    start_line(1, end_plane(1, 8))
    norms = jnp.zeros((1, 128), F32)
    v, shared, prices, norms = settle(end_line(0, 8), jnp.zeros((8, 256), F32), norms, 1)

    start_line(5, counts * common(v))
    advance(2)
    applied(2)
    start_plane(2, 8)
    v, shared, prices, norms = settle(end_line(1, 8) + end_line(5, 8), prices, norms, 2)

    start_line(6, counts * common(v))
    advance(3)
    applied(3)
    start_plane(3, 8)
    start_line(2, end_plane(2, 8))
    v, shared, prices, norms = settle(end_line(2, 8) + end_line(6, 8), prices, norms, 3)

    start_line(7, counts * common(v))
    start_line(3, end_plane(3, 8))
    advance(4)
    applied(4, summed=False)
    v, shared, prices, norms = settle(end_line(3, 8) + end_line(7, 8), prices, norms, 4)

    common(v)
    advance(5, last=True)
    for e in (1, 7, 2):
        back_copy(e).start()
    plane[4, place, 13:] = jnp.zeros((3, 256), F32)
    start_plane(4, 16)
    back[kind] = usage[z, pl.ds(pl.multiple_of(c * 64, 64), 64)]
    start_line(4, end_plane(4, 16))
    for e in (1, 7, 2):
        back_copy(e).wait_recv()
    result = jnp.zeros((256, 256), F32)
    for piece in three_parts(back[...].reshape(256, 256)):
        result += lax.dot_general(
            order[...], piece.astype(BF16), (((0,), (0,)), ((), ())), preferred_element_type=F32
        )
    usage_out[...] = result
    total = end_line(4, 16)
    v, shared, prices, norms = settle(total[:8], prices, norms, 5)
    duals = jnp.zeros((1, 128), F32)
    for k in range(ITERS):
        duals = jnp.where(norm_lane == k, jnp.sum(total[8 + k : 9 + k]), duals)
    vectors[2] = shared
    vectors[3] = prices
    small_out[0:1] = vectors[2, pl.ds(z, 1)]
    small_out[1:2] = vectors[3, pl.ds(z, 1)]
    small_out[2:3, :128] = jnp.sqrt(norms + EPS)
    small_out[3:4, :128] = jnp.sqrt(duals + EPS)

    def end_sends(e, carry):
        for k, tall in enumerate((16, 8, 8, 8, 16)):
            plane_copy(k, tall, e).wait_send()
        return carry

    lax.fori_loop(1, 16, end_sends, 0)
    for k, tall in enumerate((8, 8, 8, 8, 16, 8, 8, 8)):
        for e in range(3):
            line_copy(k, tall, e).wait_send()
    for d in range(8):
        hand_copy(d).wait_send()
    for d in range(1, 8):
        row_copy(d).wait_send()
        z_copy(d).wait_send()
        for s in (1, 2, 3):
            one_copy(d, s).wait_send()
            two_copy(d, s).wait_send()
        core_copy(d).wait_send()
    for e in (1, 7, 2):
        back_copy(e).wait_send()


def on_device(linear_cost, agent_type, block_mask, inverses, cost_weight, target):
    vmem = pl.BlockSpec(memory_space=pltpu.VMEM)
    dma = pltpu.SemaphoreType.DMA
    usage, small = pl.pallas_call(
        kernel,
        out_shape=(jax.ShapeDtypeStruct((256, 256), F32), jax.ShapeDtypeStruct((4, 256), F32)),
        in_specs=[vmem] * 5 + [pl.BlockSpec(memory_space=pl.ANY)],
        out_specs=(vmem,) * 2,
        scratch_shapes=[
            pltpu.VMEM((2, 8, 4, 4, 16, 1024), BF16),
            pltpu.VMEM((256, 256), BF16),
            pltpu.VMEM((4, 80, 256), BF16),
            pltpu.VMEM((8, 2, 80, 256), BF16),
            pltpu.VMEM((8, 128, 256), F32),
            pltpu.VMEM((8, 128, 256), F32),
            pltpu.VMEM((8, 128, 256), F32),
            pltpu.VMEM((128, 2048), BF16),
            pltpu.VMEM((16, 2048), BF16),
            pltpu.VMEM((5, 8, 256), F32),
            pltpu.VMEM((ITERS, 16, 16, 256), F32),
            pltpu.VMEM((8, 4, 16, 256), F32),
            pltpu.VMEM((4, 64, 256), F32),
            dma((32,)),
            dma((8,)), dma((8,)),
            dma((8, 4)), dma((8, 4)),
            dma((8, 4)), dma((8, 4)),
            dma((8,)), dma((8,)),
            dma((8,)), dma((8,)),
            dma((8,)), dma((8,)),
            dma((ITERS, 16)), dma((ITERS, 16)),
            dma((8, 3)), dma((8, 3)),
            dma((8,)), dma((8,)),
        ],
        compiler_params=pltpu.CompilerParams(
            collective_id=0, has_side_effects=True, vmem_limit_bytes=60 * 2**20
        ),
        name="admm",
    )(
        linear_cost,
        agent_type.reshape(1, -1),
        block_mask.T,
        cost_weight.reshape(1, -1),
        target.reshape(1, -1),
        inverses,
    )
    return usage, small[0], small[1], small[2, :ITERS], small[3, :ITERS]


def solution(mesh):
    placed = (
        P("agent", "res"),
        P("agent"),
        P("agent", "res"),
        P(None, "res", None),
        P("res"),
        P("res"),
    )
    return jax.shard_map(
        on_device,
        mesh=mesh,
        in_specs=placed,
        out_specs=(P("agent", "res"), P("res"), P("res"), P(), P()),
        check_vma=False,
    )
```

time: 127 us -> 105 us (0.83)
  Pallas kernels: 121 us -> 99.7 us
    pallas_call x1, Pallas kernels: 121 us -> 99.7 us  [on_device(): pl.pallas_call(kernel, out_shape=(jax.ShapeDtypeStruct((256, 256), F32),...]
    unnamed x3 -> x1, local copies, waits for them, and re-layouts: 4.13 us -> 1.67 us
    slice x0 -> x1, local copies, waits for them, and re-layouts: none -> 1.32 us  [on_device(): return (usage, small[0], small[1], small[2, :ITERS], small[3, :ITERS])]
where the time goes in v2:
time: 105 us
  Pallas kernels  99.7 us (95%)
  local copies, waits for them, and re-layouts  4.26 us (4%)
    pallas_call x1, Pallas kernels, on_device(): pl.pallas_call(kernel, out_shape=(jax.ShapeDtypeStruct((256, 256), F32),...  99.7 us

profile of v2, /device:TPU:32, one launch (start us, length us, event | category | flops | bytes accessed | tf_op | source)
XLA Modules:
  0.0 104.6 jit_solution(116888597023016737)
XLA Ops:
  0.6 99.7 %admm.1 = (f32[256,256]{1,0:T(8,128)}, f32[4,256]{1,0:T(4,128)}) custom-call(f32[256,256]{1,0:T(8,128)} %cost_ref.1, s32[1,256]{1,0:T(1,128)} %bitcast.13, s32[2,256]{1,0:T(2,128)} %bitcast.10, f32[1,256]{1,0:T(1,128)} %bitcast.14, f32[1,256]{1,0:T(1,128)} %bitcast.15, bf16[4,256,2048]{2,1,0:T(8,128)(2,1)} %inv_ref.1), custom_call_target="tpu_custom_call" | custom-call | tf_op jit(solution)/shard_map/admm/pallas_call | solution.py:383
  100.3 1.3 %fusion = (f32[1,256]{1,0:T(1,128)}, f32[1,256]{1,0:T(1,128)}) fusion(f32[4,256]{1,0:T(4,128)} %get-tuple-element.8), kind=kLoop, calls=%fused_computation.2 | loop fusion | bytes 4096 | tf_op jit(solution)/shard_map/slice | solution.py:425
  101.6 1.3 %slice_bitcast_fusion = (f32[5]{0:T(128)}, f32[5]{0:T(128)}) fusion(f32[4,256]{1,0:T(4,128)} %get-tuple-element.8), kind=kLoop, calls=%fused_computation | loop fusion | bytes 80 | tf_op jit(solution)/shard_map/squeeze | solution.py:425
  102.9 1.7 %copy.12 = f32[256,256]{1,0:T(8,128)} copy(f32[256,256]{1,0:T(8,128)} %get-tuple-element.18) | data formatting | bytes 524288

commit v3 on v2

--- a/solution.py
+++ b/solution.py
@@ -25,8 +25,8 @@
 def kernel(
     cost_ref, type_ref, mask_ref, weight_ref, target_ref, inv_ref,
     usage_out, small_out,
-    mats, order, packed, rows, expand, usage, others, rhs, shift, vectors, plane, lines, back,
-    mat_load, z_send, z_recv, one_send, one_recv, two_send, two_recv, core_send, core_recv,
+    stage, half, full, order, packed, rows, expand, usage, others, rhs, shift, vectors, plane, lines, back,
+    stage_load, mat_load, z_send, z_recv, one_send, one_recv, two_send, two_recv, core_send, core_recv,
     row_send, row_recv, hand_send, hand_recv, plane_send, plane_recv, line_send, line_recv, back_send, back_recv,
 ):
     agent, z = lax.axis_index("agent"), lax.axis_index("res")
@@ -59,27 +59,35 @@
     for d in range(1, 8):
         pl.semaphore_signal(barrier, inc=1, device_id=at(x, y, c, (z + d) % 8), device_id_type=MESH)
     pl.semaphore_signal(barrier, inc=1, device_id=at(x, y, 1 - c, z), device_id_type=MESH)
+    def column(k):
+        return pl.ds(pl.multiple_of(((2 * z + k) % 16) * 128, 128), 128)
+
     own_loads = [
         pltpu.make_async_copy(
-            inv_ref.at[kind, pl.ds(q * 16, 16), pl.ds(h * 1024, 1024)],
-            mats.at[h, z, q // 4, q % 4],
-            mat_load.at[h * 16 + q],
+            inv_ref.at[t, first, second, :, column(c * 5 + i)],
+            stage.at[t, :, pl.ds(i * 128, 128)],
+            stage_load.at[t * 5 + i],
         )
-        for h in range(2)
-        for q in range(16)
+        for t in range(4)
+        for i in range(5)
+    ] + [
+        pltpu.make_async_copy(
+            inv_ref.at[kind, :, :, :, column(k)],
+            half.at[k // 5, z, :, :, :, pl.ds((k % 5) * 128, 128)],
+            mat_load.at[k],
+        )
+        for k in range(10)
     ]
     for load in own_loads:
         load.start()
+    for load in own_loads[:20]:
+        load.wait()
     pl.semaphore_wait(barrier, 23)
 
     def z_copy(d):
         far = (z + d) % 8
         return copy(
-            inv_ref.at[far % 4, pl.ds((first * 4 + second) * 16, 16), pl.ds(pl.multiple_of(c * 1024, 1024), 1024)],
-            mats.at[c, z, first, second],
-            z_send.at[d],
-            z_recv.at[d],
-            at(x, y, c, far),
+            stage.at[far % 4], half.at[c, z, first, second], z_send.at[d], z_recv.at[d], at(x, y, c, far)
         )
 
     for d in (4, 3, 5, 2, 6, 1, 7):
@@ -122,7 +130,7 @@
     hand_copy(0).start()
 
     def part(d):
-        return mats.at[c, (z - d + 8) % 8]
+        return half.at[c, (z - d + 8) % 8]
 
     def one_copy(d, s):
         block = part(d).at[first, second]
@@ -155,19 +163,32 @@
         ends = rows[j, 0, 64:].astype(F32)
         vectors[0, j : j + 1] = ends[2:3] + ends[3:4] + ends[4:5]
         vectors[1, j : j + 1] = ends[5:6] + ends[6:7] + ends[7:8]
-        for half in range(2):
-            here = rows[j, half, 64:, :128]
+        for side in range(2):
+            here = rows[j, side, 64:, :128]
             spread = lax.dot_general(here, wide, (((0,), (0,)), ((), ())), preferred_element_type=F32)
-            expand[j, half * 64 : half * 64 + 64] = spread[:64]
-
-    for d in (1, 7, 2, 6, 3, 5, 4):
-        for s in (2, 1, 3):
-            two_copy(d, s).wait_recv()
-        core_copy(d).start()
-    for load in own_loads:
+            expand[j, side * 64 : side * 64 + 64] = spread[:64]
+
+    def fill(block):
+        for k in range(10):
+            tile = half[k // 5, block, :, :, :, (k % 5) * 128 : (k % 5) * 128 + 128].reshape(256, 128)
+            across = (block + k // 2) % 8
+            full[across, pl.ds(pl.multiple_of(block * 256, 256), 256), (k % 2) * 128 : (k % 2) * 128 + 128] = tile
+            if 2 <= k < 8:
+                full[block, pl.ds(pl.multiple_of(across * 256 + (k % 2) * 128, 128), 128), :] = tile.T
+
+    for load in own_loads[20:]:
         load.wait()
-    for d in (1, 7, 2, 6, 3, 5, 4):
-        core_copy(d).wait_recv()
+    fill(z)
+    ahead_of = 0
+    for d in (1, 7, 2, 6, 3, 5, 4, 0):
+        if d:
+            for s in (2, 1, 3):
+                two_copy(d, s).wait_recv()
+            core_copy(d).start()
+        if ahead_of:
+            core_copy(ahead_of).wait_recv()
+            fill((z - ahead_of + 8) % 8)
+        ahead_of = d
 
     norm_lane = lax.broadcasted_iota(jnp.int32, (1, 128), 1)
 
@@ -219,7 +240,7 @@
         return jnp.sum(lines[k, :, :tall], axis=0)
 
     def block_of(j):
-        return mats[j // 4, :, :, :, :, pl.ds(pl.multiple_of((j % 4) * 256, 256), 256)].reshape(2048, 256)
+        return full[j]
 
     def lanes_of(j):
         return pl.ds(pl.multiple_of(j * 256, 256), 256)
@@ -230,12 +251,11 @@
     def product(j):
         return jnp.dot(rhs[...], block_of(j), preferred_element_type=F32)
 
-    def applied(k, summed=True):
+    def applied(k):
         def step(j, carry):
             fresh = product(j)
             others[j] = fresh
-            if summed:
-                place_columns(k, j, fresh * expand[j])
+            place_columns(k, j, fresh * expand[j])
             return carry
 
         lax.fori_loop(0, 8, step, 0)
@@ -254,15 +274,12 @@
         lax.fori_loop(0, 8, step, 0)
         return vectors[4]
 
-    def advance(k, last=False):
+    def advance(k):
         def step(j, change):
             fresh = (others[j] + vectors[4, pl.ds(j, 1)]) * expand[j]
             gap = fresh - usage[j]
             usage[j] = fresh
-            if last:
-                place_columns(4, j, fresh)
-            else:
-                rhs[:, lanes_of(j)] = (fresh - costs_of(j)).astype(BF16)
+            rhs[:, lanes_of(j)] = (fresh - costs_of(j)).astype(BF16)
             return change + jnp.sum(gap * gap, axis=0, keepdims=True)
 
         change = lax.fori_loop(0, 8, step, jnp.zeros((1, 256), F32))
@@ -324,11 +341,23 @@
     start_line(7, counts * common(v))
     start_line(3, end_plane(3, 8))
     advance(4)
-    applied(4, summed=False)
     v, shared, prices, norms = settle(end_line(3, 8) + end_line(7, 8), prices, norms, 4)
 
-    common(v)
-    advance(5, last=True)
+    vectors[4] = v
+
+    def last_side(j, carry):
+        rhs[:, lanes_of(j)] = (usage[j] + vectors[4, pl.ds(j, 1)] - costs_of(j)).astype(BF16)
+        return carry
+
+    def closing(j, change):
+        fresh = product(j) * expand[j]
+        gap = fresh - usage[j]
+        usage[j] = fresh
+        place_columns(4, j, fresh)
+        return change + jnp.sum(gap * gap, axis=0, keepdims=True)
+
+    lax.fori_loop(0, 8, last_side, 0)
+    plane[4, place, 12:13] = lax.fori_loop(0, 8, closing, jnp.zeros((1, 256), F32))
     for e in (1, 7, 2):
         back_copy(e).start()
     plane[4, place, 13:] = jnp.zeros((3, 256), F32)
@@ -386,7 +415,9 @@
         in_specs=[vmem] * 5 + [pl.BlockSpec(memory_space=pl.ANY)],
         out_specs=(vmem,) * 2,
         scratch_shapes=[
-            pltpu.VMEM((2, 8, 4, 4, 16, 1024), BF16),
+            pltpu.VMEM((4, 16, 640), BF16),
+            pltpu.VMEM((2, 8, 4, 4, 16, 640), BF16),
+            pltpu.VMEM((8, 2048, 256), BF16),
             pltpu.VMEM((256, 256), BF16),
             pltpu.VMEM((4, 80, 256), BF16),
             pltpu.VMEM((8, 2, 80, 256), BF16),
@@ -399,7 +430,7 @@
             pltpu.VMEM((ITERS, 16, 16, 256), F32),
             pltpu.VMEM((8, 4, 16, 256), F32),
             pltpu.VMEM((4, 64, 256), F32),
-            dma((32,)),
+            dma((20,)), dma((10,)),
             dma((8,)), dma((8,)),
             dma((8, 4)), dma((8, 4)),
             dma((8, 4)), dma((8, 4)),
@@ -420,7 +451,7 @@
         block_mask.T,
         cost_weight.reshape(1, -1),
         target.reshape(1, -1),
-        inverses,
+        inverses.reshape(4, 4, 4, 16, 2048),
     )
     return usage, small[0], small[1], small[2, :ITERS], small[3, :ITERS]
 

time: 105 us -> 94.3 us (0.90)
  Pallas kernels: 99.7 us -> 89.2 us
    pallas_call x1, Pallas kernels: 99.7 us -> 89.2 us  [on_device(): pl.pallas_call(kernel, out_shape=(jax.ShapeDtypeStruct((256, 256), F32),...]
where the time goes in v3:
time: 94.3 us; the launch traced here: 94.1 us
  Pallas kernels  89.2 us (95%)
  local copies, waits for them, and re-layouts  4.26 us (5%)
    pallas_call x1, Pallas kernels, on_device(): pl.pallas_call(kernel, out_shape=(jax.ShapeDtypeStruct((256, 256), F32),...  89.2 us

profile of v3, /device:TPU:32, one launch (start us, length us, event | category | flops | bytes accessed | tf_op | source)
XLA Modules:
  0.0 94.1 jit_solution(12456146744664402587)
XLA Ops:
  0.6 89.2 %admm.1 = (f32[256,256]{1,0:T(8,128)}, f32[4,256]{1,0:T(4,128)}) custom-call(f32[256,256]{1,0:T(8,128)} %cost_ref.1, s32[1,256]{1,0:T(1,128)} %bitcast.15, s32[2,256]{1,0:T(2,128)} %bitcast.12, f32[1,256]{1,0:T(1,128)} %bitcast.16, f32[1,256]{1,0:T(1,128)} %bitcast.17, bf16[4,4,4,16,2048]{4,3,2,1,0:T(8,128)(2,1)} %bitcast.11), custom_call_target="tpu_custom_call" | custom-call | tf_op jit(solution)/shard_map/admm/pallas_call | solution.py:412
  89.8 1.3 %fusion = (f32[1,256]{1,0:T(1,128)}, f32[1,256]{1,0:T(1,128)}) fusion(f32[4,256]{1,0:T(4,128)} %get-tuple-element.8), kind=kLoop, calls=%fused_computation.2 | loop fusion | bytes 4096 | tf_op jit(solution)/shard_map/slice | solution.py:456
  91.1 1.3 %slice_bitcast_fusion = (f32[5]{0:T(128)}, f32[5]{0:T(128)}) fusion(f32[4,256]{1,0:T(4,128)} %get-tuple-element.8), kind=kLoop, calls=%fused_computation | loop fusion | bytes 80 | tf_op jit(solution)/shard_map/squeeze | solution.py:456
  92.4 1.7 %copy.12 = f32[256,256]{1,0:T(8,128)} copy(f32[256,256]{1,0:T(8,128)} %get-tuple-element.18) | data formatting | bytes 524288

commit v4 on v3

--- a/solution.py
+++ b/solution.py
@@ -8,6 +8,8 @@
 from jax.sharding import PartitionSpec as P
 
 ITERS = 5
+LAG_TWO, LAG_THREE, LAG_FOUR = 3, 6, 7
+LAST_STEP = LAG_FOUR + 7
 AGENTS = 8192
 EPS = 1e-06
 MESH = pl.DeviceIdType.MESH
@@ -25,7 +27,7 @@
 def kernel(
     cost_ref, type_ref, mask_ref, weight_ref, target_ref, inv_ref,
     usage_out, small_out,
-    stage, half, full, order, packed, rows, expand, usage, others, rhs, shift, vectors, plane, lines, back,
+    stage, half, full, order, packed, rows, expand, usage, rhs, plain, counts, vectors, plane, lines, back,
     stage_load, mat_load, z_send, z_recv, one_send, one_recv, two_send, two_recv, core_send, core_recv,
     row_send, row_recv, hand_send, hand_recv, plane_send, plane_recv, line_send, line_recv, back_send, back_recv,
 ):
@@ -58,7 +60,8 @@
     lax.fori_loop(1, 16, greet, 0)
     for d in range(1, 8):
         pl.semaphore_signal(barrier, inc=1, device_id=at(x, y, c, (z + d) % 8), device_id_type=MESH)
-    pl.semaphore_signal(barrier, inc=1, device_id=at(x, y, 1 - c, z), device_id_type=MESH)
+    for d in (0, 1, 7, 2, 6):
+        pl.semaphore_signal(barrier, inc=1, device_id=at(x, y, 1 - c, (z + d) % 8), device_id_type=MESH)
     def column(k):
         return pl.ds(pl.multiple_of(((2 * z + k) % 16) * 128, 128), 128)
 
@@ -80,18 +83,12 @@
     ]
     for load in own_loads:
         load.start()
-    for load in own_loads[:20]:
-        load.wait()
-    pl.semaphore_wait(barrier, 23)
-
     def z_copy(d):
         far = (z + d) % 8
         return copy(
             stage.at[far % 4], half.at[c, z, first, second], z_send.at[d], z_recv.at[d], at(x, y, c, far)
         )
 
-    for d in (4, 3, 5, 2, 6, 1, 7):
-        z_copy(d).start()
 
     kinds = type_ref[...]
     is_kind = (lax.broadcasted_iota(jnp.int32, (16, 256), 0) == kinds).astype(F32)
@@ -124,6 +121,11 @@
         block = rows.at[(z - d + 8) % 8, c]
         return copy(block, block, hand_send.at[d], hand_recv.at[d], at(x, y, 1 - c, z))
 
+    for load in own_loads[:20]:
+        load.wait()
+    pl.semaphore_wait(barrier, 27)
+    for d in (4, 3, 5, 2, 6, 1, 7):
+        z_copy(d).start()
     for d in (4, 3, 5, 2, 6, 1, 7):
         row_copy(d).start()
     rows[z, c] = packed[kind]
@@ -143,30 +145,8 @@
     def core_copy(d):
         return copy(part(d), part(d), core_send.at[d], core_recv.at[d], at(x, y, 1 - c, z))
 
-    for d in (1, 7, 2, 6, 3, 5, 4):
-        z_copy(d).wait_recv()
-        for s in (2, 1, 3):
-            one_copy(d, s).start()
-    for d in (1, 7, 2, 6, 3, 5, 4):
-        for s in (2, 1, 3):
-            one_copy(d, s).wait_recv()
-        for s in (2, 1, 3):
-            two_copy(d, s).start()
-    for d in (1, 7, 2, 6, 3, 5, 4):
-        row_copy(d).wait_recv()
-        hand_copy(d).start()
-
-    for d in range(8):
-        hand_copy(d).wait_recv()
+    line = lax.broadcasted_iota(jnp.int32, (16, 256), 0)
     wide = (lax.broadcasted_iota(jnp.int32, (16, 256), 1) // 128 == line).astype(F32).astype(BF16)
-    for j in range(8):
-        ends = rows[j, 0, 64:].astype(F32)
-        vectors[0, j : j + 1] = ends[2:3] + ends[3:4] + ends[4:5]
-        vectors[1, j : j + 1] = ends[5:6] + ends[6:7] + ends[7:8]
-        for side in range(2):
-            here = rows[j, side, 64:, :128]
-            spread = lax.dot_general(here, wide, (((0,), (0,)), ((), ())), preferred_element_type=F32)
-            expand[j, side * 64 : side * 64 + 64] = spread[:64]
 
     def fill(block):
         for k in range(10):
@@ -176,19 +156,51 @@
             if 2 <= k < 8:
                 full[block, pl.ds(pl.multiple_of(across * 256 + (k % 2) * 128, 128), 128), :] = tile.T
 
-    for load in own_loads[20:]:
-        load.wait()
-    fill(z)
-    ahead_of = 0
-    for d in (1, 7, 2, 6, 3, 5, 4, 0):
-        if d:
-            for s in (2, 1, 3):
-                two_copy(d, s).wait_recv()
-            core_copy(d).start()
-        if ahead_of:
-            core_copy(ahead_of).wait_recv()
-            fill((z - ahead_of + 8) % 8)
-        ahead_of = d
+    def stage_one(d):
+        z_copy(d).wait_recv()
+        for s in (2, 1, 3):
+            one_copy(d, s).start()
+
+    def stage_two(d):
+        for s in (2, 1, 3):
+            one_copy(d, s).wait_recv()
+        for s in (2, 1, 3):
+            two_copy(d, s).start()
+
+    def stage_three(d):
+        for s in (2, 1, 3):
+            two_copy(d, s).wait_recv()
+        core_copy(d).start()
+
+    def stage_four(d):
+        core_copy(d).wait_recv()
+        fill((z - d + 8) % 8)
+
+    def unpack():
+        for d in (1, 7, 2, 6, 3, 5, 4):
+            row_copy(d).wait_recv()
+            hand_copy(d).start()
+        for load in own_loads[20:]:
+            load.wait()
+        fill(z)
+        for d in range(8):
+            hand_copy(d).wait_recv()
+        for j in range(8):
+            ends = rows[j, 0, 64:].astype(F32)
+            vectors[0, j : j + 1] = ends[2:3] + ends[3:4] + ends[4:5]
+            vectors[1, j : j + 1] = ends[5:6] + ends[6:7] + ends[7:8]
+            for side in range(2):
+                here = rows[j, side, 64:, :128]
+                spread = lax.dot_general(here, wide, (((0,), (0,)), ((), ())), preferred_element_type=F32)
+                expand[j, side * 64 : side * 64 + 64] = spread[:64]
+
+    turns = (1, 7, 2, 6, 3, 5, 4)
+    for step in range(LAST_STEP):
+        for lag, act in ((0, stage_one), (LAG_TWO, stage_two), (LAG_THREE, stage_three), (LAG_FOUR, stage_four)):
+            if 0 <= step - lag < 7:
+                act(turns[step - lag])
+        if step == 8:
+            unpack()
 
     norm_lane = lax.broadcasted_iota(jnp.int32, (1, 128), 1)
 
@@ -210,33 +222,49 @@
         return copy(block, block, plane_send.at[k, e], plane_recv.at[k, e], plane_peer(e))
 
     def start_plane(k, tall):
-        def start(e, carry):
-            plane_copy(k, tall, e).start()
-            return carry
-
-        lax.fori_loop(1, 16, start, 0)
-
-    def end_plane(k, tall):
-        def end(e, carry):
-            plane_copy(k, tall, e).wait_recv()
-            return carry
-
-        lax.fori_loop(1, 16, end, 0)
-        return jnp.sum(plane[k, :, :tall], axis=0)
-
-    def line_copy(k, tall, e):
+        @pl.when(c == 1)
+        def _():
+            def start(e, carry):
+                plane_copy(k, tall, e).start()
+                return carry
+
+            lax.fori_loop(1, 16, start, 0)
+
+    def line_copy(k, tall, i):
+        e = i // 2
+        far = at(x, y, 1 - c, z) if e == 3 else at(x, y, 1 - i % 2, (z + (1, 7, 2)[e]) % 8)
         block = lines.at[k, kind, pl.ds(0, tall)]
-        return copy(block, block, line_send.at[k, e], line_recv.at[k, e], at(x, y, c, (z + (1, 7, 2)[e]) % 8))
+        return copy(block, block, line_send.at[k, i], line_recv.at[k, e], far)
 
     def start_line(k, value):
         tall = value.shape[0]
         lines[k, kind, :tall] = value
-        for e in range(3):
-            line_copy(k, tall, e).start()
+        for i in range(7):
+            line_copy(k, tall, i).start()
+
+    def relay(k, tall):
+        @pl.when(c == 1)
+        def _():
+            def end(e, carry):
+                plane_copy(k, tall, e).wait_recv()
+                return carry
+
+            lax.fori_loop(1, 16, end, 0)
+            sums = jnp.sum(plane[k, :, :tall], axis=0)
+            if k == 1:
+                start_line(k, sums[:8])
+                counts[...] = sums[8:]
+            else:
+                start_line(k, sums)
 
     def end_line(k, tall):
         for e in range(3):
-            line_copy(k, tall, e).wait_recv()
+            line_copy(k, tall, 2 * e).wait_recv()
+
+        @pl.when(c == 0)
+        def _():
+            line_copy(k, tall, 6).wait_recv()
+
         return jnp.sum(lines[k, :, :tall], axis=0)
 
     def block_of(j):
@@ -248,42 +276,47 @@
     def costs_of(j):
         return rows[j, :, :64].astype(F32).reshape(128, 256)
 
-    def product(j):
-        return jnp.dot(rhs[...], block_of(j), preferred_element_type=F32)
+    def opened(j):
+        return jnp.dot(plain[...], block_of(j), preferred_element_type=F32)
 
     def applied(k):
         def step(j, carry):
-            fresh = product(j)
-            others[j] = fresh
-            place_columns(k, j, fresh * expand[j])
+            place_columns(k, j, opened(j) * expand[j])
             return carry
 
-        lax.fori_loop(0, 8, step, 0)
-
-    def common(v):
-        high, mid, low = three_parts(v)
+        lax.fori_loop(0, 8, step, 0, unroll=2)
+
+    def advance(k, v, ex=None):
+        vectors[4] = v
         for j in range(8):
-            stack = jnp.where(line == 0, high[j : j + 1], jnp.where(line == 1, mid[j : j + 1], low[j : j + 1]))
-            shift[:, j * 256 : (j + 1) * 256] = jnp.where(line < 3, stack, 0.0).astype(BF16)
-
-        def step(j, carry):
-            out = jnp.dot(shift[...], block_of(j), preferred_element_type=F32)
-            vectors[4, pl.ds(j, 1)] = out[0:1] + out[1:2] + out[2:3]
-            return carry
-
-        lax.fori_loop(0, 8, step, 0)
-        return vectors[4]
-
-    def advance(k):
+            rhs[:128, j * 256 : (j + 1) * 256] = (usage[j] + vectors[4, j : j + 1] - costs_of(j)).astype(BF16)
+        if ex is not None:
+            high, mid, low = three_parts(v)
+            for j in range(8):
+                stack = jnp.where(line == 0, high[j : j + 1], jnp.where(line == 1, mid[j : j + 1], low[j : j + 1]))
+                rhs[128:, j * 256 : (j + 1) * 256] = jnp.where(line < 3, stack, 0.0).astype(BF16)
+
         def step(j, change):
-            fresh = (others[j] + vectors[4, pl.ds(j, 1)]) * expand[j]
+            if ex is None:
+                fresh = jnp.dot(rhs[:128], block_of(j), preferred_element_type=F32)
+            else:
+                both = jnp.dot(rhs[...], block_of(j), preferred_element_type=F32)
+                vectors[4, pl.ds(j, 1)] = both[128:129] + both[129:130] + both[130:131]
+                fresh = both[:128]
+            fresh = fresh * expand[j]
             gap = fresh - usage[j]
             usage[j] = fresh
-            rhs[:, lanes_of(j)] = (fresh - costs_of(j)).astype(BF16)
+            if ex is None:
+                place_columns(4, j, fresh)
+            else:
+                plain[:, lanes_of(j)] = (fresh - costs_of(j)).astype(BF16)
             return change + jnp.sum(gap * gap, axis=0, keepdims=True)
 
-        change = lax.fori_loop(0, 8, step, jnp.zeros((1, 256), F32))
-        plane[4, place, 7 + k : 8 + k] = change
+        plane[4, place, 7 + k : 8 + k] = lax.fori_loop(0, 8, step, jnp.zeros((1, 256), F32), unroll=2)
+        if ex is not None:
+            @pl.when(c == 1)
+            def _():
+                start_line(ex, counts[...] * vectors[4])
 
     def settle(total, prices, norms, k):
         mean = total * (1.0 / AGENTS)
@@ -293,77 +326,45 @@
         norms = jnp.where(norm_lane == k - 1, float(AGENTS) * jnp.sum(gap * gap), norms)
         return shared - mean - prices, shared, prices, norms
 
-    def negated(j, carry):
-        rhs[:, lanes_of(j)] = -rows[j, :, :64].reshape(128, 256)
-        return carry
-
-    lax.fori_loop(0, 8, negated, 0)
+    for j in range(8):
+        rhs[:128, j * 256 : (j + 1) * 256] = -rows[j, :, :64].reshape(128, 256)
 
     def opening(j, change):
-        fresh = product(j) * expand[j]
+        fresh = jnp.dot(rhs[:128], block_of(j), preferred_element_type=F32) * expand[j]
         usage[j] = fresh
+        plain[:, lanes_of(j)] = (fresh - costs_of(j)).astype(BF16)
         place_columns(0, j, fresh)
         return change + jnp.sum(fresh * fresh, axis=0, keepdims=True)
 
-    change = lax.fori_loop(0, 8, opening, jnp.zeros((1, 256), F32))
-    plane[4, place, 8:9] = change
+    plane[4, place, 8:9] = lax.fori_loop(0, 8, opening, jnp.zeros((1, 256), F32), unroll=2)
+    start_plane(0, 8)
     for j in range(8):
-        plane[0, place, 8 + j : 9 + j] = jnp.sum(expand[j], axis=0, keepdims=True)
-    start_plane(0, 16)
-
-    def second_side(j, carry):
-        rhs[:, lanes_of(j)] = (usage[j] - costs_of(j)).astype(BF16)
-        return carry
-
-    lax.fori_loop(0, 8, second_side, 0)
+        plane[1, place, 8 + j : 9 + j] = jnp.sum(expand[j], axis=0, keepdims=True)
     applied(1)
-    start_plane(1, 8)
-    sums = end_plane(0, 16)
-    start_line(0, sums[:8])
-    counts = sums[8:]
-    start_line(1, end_plane(1, 8))
+    start_plane(1, 16)
+    relay(0, 8)
+    relay(1, 16)
     norms = jnp.zeros((1, 128), F32)
     v, shared, prices, norms = settle(end_line(0, 8), jnp.zeros((8, 256), F32), norms, 1)
-
-    start_line(5, counts * common(v))
-    advance(2)
+    advance(2, v, ex=5)
     applied(2)
     start_plane(2, 8)
     v, shared, prices, norms = settle(end_line(1, 8) + end_line(5, 8), prices, norms, 2)
-
-    start_line(6, counts * common(v))
-    advance(3)
+    advance(3, v, ex=6)
     applied(3)
     start_plane(3, 8)
-    start_line(2, end_plane(2, 8))
+    relay(2, 8)
     v, shared, prices, norms = settle(end_line(2, 8) + end_line(6, 8), prices, norms, 3)
-
-    start_line(7, counts * common(v))
-    start_line(3, end_plane(3, 8))
-    advance(4)
+    advance(4, v, ex=7)
+    relay(3, 8)
     v, shared, prices, norms = settle(end_line(3, 8) + end_line(7, 8), prices, norms, 4)
-
-    vectors[4] = v
-
-    def last_side(j, carry):
-        rhs[:, lanes_of(j)] = (usage[j] + vectors[4, pl.ds(j, 1)] - costs_of(j)).astype(BF16)
-        return carry
-
-    def closing(j, change):
-        fresh = product(j) * expand[j]
-        gap = fresh - usage[j]
-        usage[j] = fresh
-        place_columns(4, j, fresh)
-        return change + jnp.sum(gap * gap, axis=0, keepdims=True)
-
-    lax.fori_loop(0, 8, last_side, 0)
-    plane[4, place, 12:13] = lax.fori_loop(0, 8, closing, jnp.zeros((1, 256), F32))
+    advance(5, v)
     for e in (1, 7, 2):
         back_copy(e).start()
     plane[4, place, 13:] = jnp.zeros((3, 256), F32)
     start_plane(4, 16)
     back[kind] = usage[z, pl.ds(pl.multiple_of(c * 64, 64), 64)]
-    start_line(4, end_plane(4, 16))
+    relay(4, 16)
     for e in (1, 7, 2):
         back_copy(e).wait_recv()
     result = jnp.zeros((256, 256), F32)
@@ -384,15 +385,18 @@
     small_out[2:3, :128] = jnp.sqrt(norms + EPS)
     small_out[3:4, :128] = jnp.sqrt(duals + EPS)
 
-    def end_sends(e, carry):
-        for k, tall in enumerate((16, 8, 8, 8, 16)):
-            plane_copy(k, tall, e).wait_send()
-        return carry
-
-    lax.fori_loop(1, 16, end_sends, 0)
-    for k, tall in enumerate((8, 8, 8, 8, 16, 8, 8, 8)):
-        for e in range(3):
-            line_copy(k, tall, e).wait_send()
+    @pl.when(c == 1)
+    def _():
+        def end_sends(e, carry):
+            for k, tall in enumerate((8, 16, 8, 8, 16)):
+                plane_copy(k, tall, e).wait_send()
+            return carry
+
+        lax.fori_loop(1, 16, end_sends, 0)
+        for k, tall in enumerate((8, 8, 8, 8, 16, 8, 8, 8)):
+            for i in range(7):
+                line_copy(k, tall, i).wait_send()
+
     for d in range(8):
         hand_copy(d).wait_send()
     for d in range(1, 8):
@@ -423,9 +427,9 @@
             pltpu.VMEM((8, 2, 80, 256), BF16),
             pltpu.VMEM((8, 128, 256), F32),
             pltpu.VMEM((8, 128, 256), F32),
-            pltpu.VMEM((8, 128, 256), F32),
+            pltpu.VMEM((144, 2048), BF16),
             pltpu.VMEM((128, 2048), BF16),
-            pltpu.VMEM((16, 2048), BF16),
+            pltpu.VMEM((8, 256), F32),
             pltpu.VMEM((5, 8, 256), F32),
             pltpu.VMEM((ITERS, 16, 16, 256), F32),
             pltpu.VMEM((8, 4, 16, 256), F32),
@@ -438,7 +442,7 @@
             dma((8,)), dma((8,)),
             dma((8,)), dma((8,)),
             dma((ITERS, 16)), dma((ITERS, 16)),
-            dma((8, 3)), dma((8, 3)),
+            dma((8, 7)), dma((8, 4)),
             dma((8,)), dma((8,)),
         ],
         compiler_params=pltpu.CompilerParams(

time: 94.3 us -> 88.4 us (0.937); the launches traced: 94.1 us -> 87.2 us
  Pallas kernels: 89.2 us -> 82.3 us
    pallas_call x1, Pallas kernels: 89.2 us -> 82.3 us  [on_device(): pl.pallas_call(kernel, out_shape=(jax.ShapeDtypeStruct((256, 256), F32),...]
where the time goes in v4:
time: 88.4 us; the launch traced here: 87.2 us
  Pallas kernels  82.3 us (93%)
  local copies, waits for them, and re-layouts  4.26 us (5%)
    pallas_call x1, Pallas kernels, on_device(): pl.pallas_call(kernel, out_shape=(jax.ShapeDtypeStruct((256, 256), F32),...  82.3 us

profile of v4, /device:TPU:32, one launch (start us, length us, event | category | flops | bytes accessed | tf_op | source)
XLA Modules:
  0.0 87.2 jit_solution(5754254642587166757)
XLA Ops:
  0.6 82.3 %admm.1 = (f32[256,256]{1,0:T(8,128)}, f32[4,256]{1,0:T(4,128)}) custom-call(f32[256,256]{1,0:T(8,128)} %cost_ref.1, s32[1,256]{1,0:T(1,128)} %bitcast.15, s32[2,256]{1,0:T(2,128)} %bitcast.12, f32[1,256]{1,0:T(1,128)} %bitcast.16, f32[1,256]{1,0:T(1,128)} %bitcast.17, bf16[4,4,4,16,2048]{4,3,2,1,0:T(8,128)(2,1)} %bitcast.11), custom_call_target="tpu_custom_call" | custom-call | tf_op jit(solution)/shard_map/admm/pallas_call | solution.py:416
  82.9 1.3 %fusion = (f32[1,256]{1,0:T(1,128)}, f32[1,256]{1,0:T(1,128)}) fusion(f32[4,256]{1,0:T(4,128)} %get-tuple-element.8), kind=kLoop, calls=%fused_computation.2 | loop fusion | bytes 4096 | tf_op jit(solution)/shard_map/slice | solution.py:460
  84.3 1.3 %slice_bitcast_fusion = (f32[5]{0:T(128)}, f32[5]{0:T(128)}) fusion(f32[4,256]{1,0:T(4,128)} %get-tuple-element.8), kind=kLoop, calls=%fused_computation | loop fusion | bytes 80 | tf_op jit(solution)/shard_map/squeeze | solution.py:460
  85.5 1.7 %copy.12 = f32[256,256]{1,0:T(8,128)} copy(f32[256,256]{1,0:T(8,128)} %get-tuple-element.18) | data formatting | bytes 524288

commit v5 on v4

--- a/solution.py
+++ b/solution.py
@@ -25,10 +25,10 @@
 
 
 def kernel(
-    cost_ref, type_ref, mask_ref, weight_ref, target_ref, inv_ref,
-    usage_out, small_out,
-    stage, half, full, order, packed, rows, expand, usage, rhs, plain, counts, vectors, plane, lines, back,
-    stage_load, mat_load, z_send, z_recv, one_send, one_recv, two_send, two_recv, core_send, core_recv,
+    cost_hbm, type_hbm, mask_hbm, weight_hbm, target_hbm, inv_ref,
+    usage_hbm, small_out,
+    cost_ref, type_ref, mask_ref, weight_ref, target_ref, usage_out, stage, half, full, order, packed, rows, expand, usage, rhs, plain, counts, vectors, plane, lines, back,
+    in_load, out_store, stage_load, mat_load, z_send, z_recv, one_send, one_recv, two_send, two_recv, core_send, core_recv,
     row_send, row_recv, hand_send, hand_recv, plane_send, plane_recv, line_send, line_recv, back_send, back_recv,
 ):
     agent, z = lax.axis_index("agent"), lax.axis_index("res")
@@ -65,6 +65,17 @@
     def column(k):
         return pl.ds(pl.multiple_of(((2 * z + k) % 16) * 128, 128), 128)
 
+    in_loads = [
+        pltpu.make_async_copy(src, dst, in_load.at[i])
+        for i, (src, dst) in enumerate(
+            (
+                (cost_hbm, cost_ref), (type_hbm, type_ref), (mask_hbm, mask_ref),
+                (weight_hbm, weight_ref), (target_hbm, target_ref),
+            )
+        )
+    ]
+    for load in in_loads:
+        load.start()
     own_loads = [
         pltpu.make_async_copy(
             inv_ref.at[t, first, second, :, column(c * 5 + i)],
@@ -90,6 +101,8 @@
         )
 
 
+    for load in in_loads:
+        load.wait()
     kinds = type_ref[...]
     is_kind = (lax.broadcasted_iota(jnp.int32, (16, 256), 0) == kinds).astype(F32)
     before = (
@@ -124,9 +137,9 @@
     for load in own_loads[:20]:
         load.wait()
     pl.semaphore_wait(barrier, 27)
-    for d in (4, 3, 5, 2, 6, 1, 7):
+    for d in (1, 7, 2, 6, 3, 5, 4):
         z_copy(d).start()
-    for d in (4, 3, 5, 2, 6, 1, 7):
+    for d in (1, 7, 2, 6, 3, 5, 4):
         row_copy(d).start()
     rows[z, c] = packed[kind]
     hand_copy(0).start()
@@ -156,6 +169,24 @@
             if 2 <= k < 8:
                 full[block, pl.ds(pl.multiple_of(across * 256 + (k % 2) * 128, 128), 128), :] = tile.T
 
+    def first_product(block):
+        for j in range(5):
+            across = (block + j) % 8
+            usage[across] += jnp.dot(
+                rows[block, :, :64].reshape(128, 256),
+                full[across, pl.ds(pl.multiple_of(block * 256, 256), 256), :],
+                preferred_element_type=F32,
+            )
+        mirror = jnp.zeros((128, 256), F32)
+        for j in range(1, 4):
+            across = (block + j) % 8
+            mirror += jnp.dot(
+                rows[across, :, :64].reshape(128, 256),
+                full[block, pl.ds(pl.multiple_of(across * 256, 256), 256), :],
+                preferred_element_type=F32,
+            )
+        usage[block] += mirror
+
     def stage_one(d):
         z_copy(d).wait_recv()
         for s in (2, 1, 3):
@@ -175,6 +206,7 @@
     def stage_four(d):
         core_copy(d).wait_recv()
         fill((z - d + 8) % 8)
+        first_product((z - d + 8) % 8)
 
     def unpack():
         for d in (1, 7, 2, 6, 3, 5, 4):
@@ -193,13 +225,15 @@
                 here = rows[j, side, 64:, :128]
                 spread = lax.dot_general(here, wide, (((0,), (0,)), ((), ())), preferred_element_type=F32)
                 expand[j, side * 64 : side * 64 + 64] = spread[:64]
+        usage[...] = jnp.zeros((8, 128, 256), F32)
+        first_product(z)
 
     turns = (1, 7, 2, 6, 3, 5, 4)
     for step in range(LAST_STEP):
         for lag, act in ((0, stage_one), (LAG_TWO, stage_two), (LAG_THREE, stage_three), (LAG_FOUR, stage_four)):
             if 0 <= step - lag < 7:
                 act(turns[step - lag])
-        if step == 8:
+        if step == LAG_FOUR - 1:
             unpack()
 
     norm_lane = lax.broadcasted_iota(jnp.int32, (1, 128), 1)
@@ -326,11 +360,8 @@
         norms = jnp.where(norm_lane == k - 1, float(AGENTS) * jnp.sum(gap * gap), norms)
         return shared - mean - prices, shared, prices, norms
 
-    for j in range(8):
-        rhs[:128, j * 256 : (j + 1) * 256] = -rows[j, :, :64].reshape(128, 256)
-
     def opening(j, change):
-        fresh = jnp.dot(rhs[:128], block_of(j), preferred_element_type=F32) * expand[j]
+        fresh = -usage[j] * expand[j]
         usage[j] = fresh
         plain[:, lanes_of(j)] = (fresh - costs_of(j)).astype(BF16)
         place_columns(0, j, fresh)
@@ -373,6 +404,8 @@
             order[...], piece.astype(BF16), (((0,), (0,)), ((), ())), preferred_element_type=F32
         )
     usage_out[...] = result
+    usage_store = pltpu.make_async_copy(usage_out, usage_hbm, out_store)
+    usage_store.start()
     total = end_line(4, 16)
     v, shared, prices, norms = settle(total[:8], prices, norms, 5)
     duals = jnp.zeros((1, 128), F32)
@@ -384,6 +417,7 @@
     small_out[1:2] = vectors[3, pl.ds(z, 1)]
     small_out[2:3, :128] = jnp.sqrt(norms + EPS)
     small_out[3:4, :128] = jnp.sqrt(duals + EPS)
+    usage_store.wait()
 
     @pl.when(c == 1)
     def _():
@@ -410,15 +444,30 @@
         back_copy(e).wait_send()
 
 
+def hand_over(usage_ref, small_ref, usage_out, shared_out, prices_out, primal_out, dual_out):
+    usage_out[...] = usage_ref[...]
+    shared_out[...] = small_ref[0:1]
+    prices_out[...] = small_ref[1:2]
+    primal_out[...] = small_ref[2:3, :ITERS]
+    dual_out[...] = small_ref[3:4, :ITERS]
+
+
 def on_device(linear_cost, agent_type, block_mask, inverses, cost_weight, target):
     vmem = pl.BlockSpec(memory_space=pltpu.VMEM)
+    anywhere = pl.BlockSpec(memory_space=pl.ANY)
     dma = pltpu.SemaphoreType.DMA
     usage, small = pl.pallas_call(
         kernel,
         out_shape=(jax.ShapeDtypeStruct((256, 256), F32), jax.ShapeDtypeStruct((4, 256), F32)),
-        in_specs=[vmem] * 5 + [pl.BlockSpec(memory_space=pl.ANY)],
-        out_specs=(vmem,) * 2,
+        in_specs=[anywhere] * 6,
+        out_specs=(anywhere, vmem),
         scratch_shapes=[
+            pltpu.VMEM((256, 256), F32),
+            pltpu.VMEM((1, 256), jnp.int32),
+            pltpu.VMEM((2, 256), jnp.int32),
+            pltpu.VMEM((1, 256), F32),
+            pltpu.VMEM((1, 256), F32),
+            pltpu.VMEM((256, 256), F32),
             pltpu.VMEM((4, 16, 640), BF16),
             pltpu.VMEM((2, 8, 4, 4, 16, 640), BF16),
             pltpu.VMEM((8, 2048, 256), BF16),
@@ -434,7 +483,7 @@
             pltpu.VMEM((ITERS, 16, 16, 256), F32),
             pltpu.VMEM((8, 4, 16, 256), F32),
             pltpu.VMEM((4, 64, 256), F32),
-            dma((20,)), dma((10,)),
+            dma((5,)), dma, dma((20,)), dma((10,)),
             dma((8,)), dma((8,)),
             dma((8, 4)), dma((8, 4)),
             dma((8, 4)), dma((8, 4)),
@@ -457,7 +506,20 @@
         target.reshape(1, -1),
         inverses.reshape(4, 4, 4, 16, 2048),
     )
-    return usage, small[0], small[1], small[2, :ITERS], small[3, :ITERS]
+    usage, shared, prices, primal, dual = pl.pallas_call(
+        hand_over,
+        out_shape=(
+            jax.ShapeDtypeStruct((256, 256), F32),
+            jax.ShapeDtypeStruct((1, 256), F32),
+            jax.ShapeDtypeStruct((1, 256), F32),
+            jax.ShapeDtypeStruct((1, ITERS), F32),
+            jax.ShapeDtypeStruct((1, ITERS), F32),
+        ),
+        in_specs=[vmem] * 2,
+        out_specs=(vmem,) * 5,
+        name="hand_over",
+    )(usage, small)
+    return usage, shared.reshape(-1), prices.reshape(-1), primal.reshape(-1), dual.reshape(-1)
 
 
 def solution(mesh):

time: 88.4 us -> 80.8 us (0.914)
  local copies, waits for them, and re-layouts: 4.26 us -> 0 us
  Pallas kernels: 82.3 us -> 78.9 us
    pallas_call x1, Pallas kernels: 82.3 us -> 77.3 us  [on_device(): pl.pallas_call(kernel, out_shape=(jax.ShapeDtypeStruct((256, 256), F32),...]
    pallas_call x0 -> x1, Pallas kernels: none -> 1.68 us  [on_device(): pl.pallas_call(hand_over, out_shape=(jax.ShapeDtypeStruct((256, 256), F32...]
    unnamed x1 -> x0, local copies, waits for them, and re-layouts: 1.67 us -> none
    slice x1 -> x0, local copies, waits for them, and re-layouts: 1.32 us -> none  [on_device(): return (usage, small[0], small[1], small[2, :ITERS], small[3, :ITERS])]
    squeeze x1 -> x0, local copies, waits for them, and re-layouts: 1.27 us -> none  [on_device(): return (usage, small[0], small[1], small[2, :ITERS], small[3, :ITERS])]
where the time goes in v5:
time: 80.8 us; the launch traced here: 79.6 us
  Pallas kernels  78.9 us (98%)
    pallas_call x1, Pallas kernels, on_device(): pl.pallas_call(kernel, out_shape=(jax.ShapeDtypeStruct((256, 256), F32),...  77.3 us
    pallas_call x1, Pallas kernels, on_device(): pl.pallas_call(hand_over, out_shape=(jax.ShapeDtypeStruct((256, 256), F32...  1.68 us

profile of v5, /device:TPU:32, one launch (start us, length us, event | category | flops | bytes accessed | tf_op | source)
XLA Modules:
  0.0 79.6 jit_solution(629094944203001309)
XLA Ops:
  0.6 77.3 %admm.1 = (f32[256,256]{1,0:T(8,128)}, f32[4,256]{1,0:T(4,128)}) custom-call(f32[256,256]{1,0:T(8,128)} %cost_hbm.1, s32[1,256]{1,0:T(1,128)} %bitcast.11, s32[2,256]{1,0:T(2,128)} %bitcast.10, f32[1,256]{1,0:T(1,128)} %bitcast.12, f32[1,256]{1,0:T(1,128)} %bitcast.13, bf16[4,4,4,16,2048]{4,3,2,1,0:T(8,128)(2,1)} %bitcast.9), custom_call_target="tpu_custom_call" | custom-call | tf_op jit(solution)/shard_map/admm/pallas_call | solution.py:459
  77.9 1.7 %hand_over.1 = (f32[256,256]{1,0:T(8,128)}, f32[1,256]{1,0:T(1,128)}, f32[1,256]{1,0:T(1,128)}, f32[1,5]{1,0:T(1,128)}, f32[1,5]{1,0:T(1,128)}) custom-call(f32[256,256]{1,0:T(8,128)} %get-tuple-element.12.usage_ref, f32[4,256]{1,0:T(4,128)} %get-tuple-element.13.small_ref), custom_call_target="tpu_custom_call" | custom-call | tf_op jit(solution)/shard_map/hand_over/pallas_call | solution.py:509

commit v6 on v5

--- a/solution.py
+++ b/solution.py
@@ -78,7 +78,7 @@
         load.start()
     own_loads = [
         pltpu.make_async_copy(
-            inv_ref.at[t, first, second, :, column(c * 5 + i)],
+            inv_ref.at[t, first, second, :, column(c * 4 + i + (i // 4) * (4 - 3 * c))],
             stage.at[t, :, pl.ds(i * 128, 128)],
             stage_load.at[t * 5 + i],
         )
@@ -87,19 +87,41 @@
     ] + [
         pltpu.make_async_copy(
             inv_ref.at[kind, :, :, :, column(k)],
-            half.at[k // 5, z, :, :, :, pl.ds((k % 5) * 128, 128)],
+            half.at[(k // 4 if k < 8 else k - 8), z, :, :, :, pl.ds((k % 4 if k < 8 else 4) * 128, 128)],
             mat_load.at[k],
         )
         for k in range(10)
     ]
     for load in own_loads:
         load.start()
-    def z_copy(d):
+    def sized(source, act):
+        @pl.when(source < 4)
+        def _():
+            act(640)
+
+        @pl.when(source >= 4)
+        def _():
+            act(512)
+
+    def z_copy(d, width):
         far = (z + d) % 8
         return copy(
-            stage.at[far % 4], half.at[c, z, first, second], z_send.at[d], z_recv.at[d], at(x, y, c, far)
-        )
-
+            stage.at[far % 4, :, :width],
+            half.at[c, z, first, second, :, :width],
+            z_send.at[d],
+            z_recv.at[d],
+            at(x, y, c, far),
+        )
+
+    for load in own_loads[:20]:
+        load.wait()
+    pl.semaphore_wait(barrier, 27)
+
+    def start_parts(width):
+        for d in (1, 7, 2, 6, 3, 5, 4):
+            z_copy(d, width).start()
+
+    sized(z, start_parts)
 
     for load in in_loads:
         load.wait()
@@ -134,79 +156,86 @@
         block = rows.at[(z - d + 8) % 8, c]
         return copy(block, block, hand_send.at[d], hand_recv.at[d], at(x, y, 1 - c, z))
 
-    for load in own_loads[:20]:
-        load.wait()
-    pl.semaphore_wait(barrier, 27)
-    for d in (1, 7, 2, 6, 3, 5, 4):
-        z_copy(d).start()
     for d in (1, 7, 2, 6, 3, 5, 4):
         row_copy(d).start()
     rows[z, c] = packed[kind]
     hand_copy(0).start()
 
-    def part(d):
-        return half.at[c, (z - d + 8) % 8]
-
-    def one_copy(d, s):
-        block = part(d).at[first, second]
+    def source(d):
+        return (z - d + 8) % 8
+
+    def one_copy(d, s, width):
+        block = half.at[c, source(d), first, second, :, :width]
         return copy(block, block, one_send.at[d, s], one_recv.at[d, s], along(s, 0))
 
-    def two_copy(d, s):
-        block = part(d).at[:, second]
+    def two_copy(d, s, width):
+        block = half.at[c, source(d), :, second, :, :width]
         return copy(block, block, two_send.at[d, s], two_recv.at[d, s], along(0, s))
 
-    def core_copy(d):
-        return copy(part(d), part(d), core_send.at[d], core_recv.at[d], at(x, y, 1 - c, z))
+    def core_copy(d, width):
+        block = half.at[c, source(d), :, :, :, :width]
+        return copy(block, block, core_send.at[d], core_recv.at[d], at(x, y, 1 - c, z))
 
     line = lax.broadcasted_iota(jnp.int32, (16, 256), 0)
     wide = (lax.broadcasted_iota(jnp.int32, (16, 256), 1) // 128 == line).astype(F32).astype(BF16)
 
-    def fill(block):
-        for k in range(10):
-            tile = half[k // 5, block, :, :, :, (k % 5) * 128 : (k % 5) * 128 + 128].reshape(256, 128)
+    def fill_tiles(block, picked):
+        for k in picked:
+            side, spot_ = (k // 4, k % 4) if k < 8 else (k - 8, 4)
+            tile = half[side, block, :, :, :, spot_ * 128 : spot_ * 128 + 128].reshape(256, 128)
             across = (block + k // 2) % 8
             full[across, pl.ds(pl.multiple_of(block * 256, 256), 256), (k % 2) * 128 : (k % 2) * 128 + 128] = tile
-            if 2 <= k < 8:
+            if k >= 2:
                 full[block, pl.ds(pl.multiple_of(across * 256 + (k % 2) * 128, 128), 128), :] = tile.T
 
-    def first_product(block):
-        for j in range(5):
+    def times(row_block, column_block):
+        return jnp.dot(
+            rows[row_block, :, :64].reshape(128, 256),
+            full[column_block, pl.ds(pl.multiple_of(row_block * 256, 256), 256), :],
+            preferred_element_type=F32,
+        )
+
+    def fill(block):
+        fill_tiles(block, range(8))
+        for j in range(4):
             across = (block + j) % 8
-            usage[across] += jnp.dot(
-                rows[block, :, :64].reshape(128, 256),
-                full[across, pl.ds(pl.multiple_of(block * 256, 256), 256), :],
-                preferred_element_type=F32,
-            )
+            usage[across] += times(block, across)
         mirror = jnp.zeros((128, 256), F32)
         for j in range(1, 4):
-            across = (block + j) % 8
-            mirror += jnp.dot(
-                rows[across, :, :64].reshape(128, 256),
-                full[block, pl.ds(pl.multiple_of(across * 256, 256), 256), :],
-                preferred_element_type=F32,
-            )
+            mirror += times((block + j) % 8, block)
         usage[block] += mirror
 
-    def stage_one(d):
-        z_copy(d).wait_recv()
+        @pl.when(block < 4)
+        def _():
+            across = (block + 4) % 8
+            fill_tiles(block, (8, 9))
+            usage[across] += times(block, across)
+            usage[block] += times(across, block)
+
+    def stage_one(d, width):
+        z_copy(d, width).wait_recv()
         for s in (2, 1, 3):
-            one_copy(d, s).start()
-
-    def stage_two(d):
+            one_copy(d, s, width).start()
+
+    def stage_two(d, width):
         for s in (2, 1, 3):
-            one_copy(d, s).wait_recv()
+            one_copy(d, s, width).wait_recv()
         for s in (2, 1, 3):
-            two_copy(d, s).start()
-
-    def stage_three(d):
+            two_copy(d, s, width).start()
+
+    def stage_three(d, width):
         for s in (2, 1, 3):
-            two_copy(d, s).wait_recv()
-        core_copy(d).start()
-
-    def stage_four(d):
-        core_copy(d).wait_recv()
-        fill((z - d + 8) % 8)
-        first_product((z - d + 8) % 8)
+            two_copy(d, s, width).wait_recv()
+        core_copy(d, width).start()
+
+    def stage_four(d, width):
+        core_copy(d, width).wait_recv()
+
+    def end_parts(d, width):
+        for s in (1, 2, 3):
+            one_copy(d, s, width).wait_send()
+            two_copy(d, s, width).wait_send()
+        core_copy(d, width).wait_send()
 
     def unpack():
         for d in (1, 7, 2, 6, 3, 5, 4):
@@ -214,7 +243,6 @@
             hand_copy(d).start()
         for load in own_loads[20:]:
             load.wait()
-        fill(z)
         for d in range(8):
             hand_copy(d).wait_recv()
         for j in range(8):
@@ -226,13 +254,15 @@
                 spread = lax.dot_general(here, wide, (((0,), (0,)), ((), ())), preferred_element_type=F32)
                 expand[j, side * 64 : side * 64 + 64] = spread[:64]
         usage[...] = jnp.zeros((8, 128, 256), F32)
-        first_product(z)
+        fill(z)
 
     turns = (1, 7, 2, 6, 3, 5, 4)
     for step in range(LAST_STEP):
         for lag, act in ((0, stage_one), (LAG_TWO, stage_two), (LAG_THREE, stage_three), (LAG_FOUR, stage_four)):
             if 0 <= step - lag < 7:
-                act(turns[step - lag])
+                sized(source(turns[step - lag]), functools.partial(act, turns[step - lag]))
+                if act is stage_four:
+                    fill(source(turns[step - lag]))
         if step == LAG_FOUR - 1:
             unpack()
 
@@ -322,35 +352,56 @@
 
     def advance(k, v, ex=None):
         vectors[4] = v
+        high, mid, low = three_parts(v)
         for j in range(8):
             rhs[:128, j * 256 : (j + 1) * 256] = (usage[j] + vectors[4, j : j + 1] - costs_of(j)).astype(BF16)
-        if ex is not None:
-            high, mid, low = three_parts(v)
-            for j in range(8):
-                stack = jnp.where(line == 0, high[j : j + 1], jnp.where(line == 1, mid[j : j + 1], low[j : j + 1]))
-                rhs[128:, j * 256 : (j + 1) * 256] = jnp.where(line < 3, stack, 0.0).astype(BF16)
+            stack = jnp.where(line == 0, high[j : j + 1], jnp.where(line == 1, mid[j : j + 1], low[j : j + 1]))
+            rhs[128:, j * 256 : (j + 1) * 256] = jnp.where(line < 3, stack, 0.0).astype(BF16)
 
         def step(j, change):
-            if ex is None:
-                fresh = jnp.dot(rhs[:128], block_of(j), preferred_element_type=F32)
-            else:
-                both = jnp.dot(rhs[...], block_of(j), preferred_element_type=F32)
-                vectors[4, pl.ds(j, 1)] = both[128:129] + both[129:130] + both[130:131]
-                fresh = both[:128]
-            fresh = fresh * expand[j]
+            both = jnp.dot(rhs[...], block_of(j), preferred_element_type=F32)
+            vectors[4, pl.ds(j, 1)] = both[128:129] + both[129:130] + both[130:131]
+            fresh = both[:128] * expand[j]
             gap = fresh - usage[j]
             usage[j] = fresh
-            if ex is None:
-                place_columns(4, j, fresh)
-            else:
+            if ex is not None:
                 plain[:, lanes_of(j)] = (fresh - costs_of(j)).astype(BF16)
             return change + jnp.sum(gap * gap, axis=0, keepdims=True)
 
-        plane[4, place, 7 + k : 8 + k] = lax.fori_loop(0, 8, step, jnp.zeros((1, 256), F32), unroll=2)
+        change = lax.fori_loop(0, 8, step, jnp.zeros((1, 256), F32), unroll=2)
         if ex is not None:
+            plane[4, place, 7 + k : 8 + k] = change
+
             @pl.when(c == 1)
             def _():
                 start_line(ex, counts[...] * vectors[4])
+
+    def foreseen():
+        vectors[5] = vectors[4]
+
+        def step(j, change):
+            gap = (opened(j) + vectors[5, pl.ds(j, 1)]) * expand[j] - usage[j]
+            place_columns(4, j, gap)
+            return change + jnp.sum(gap * gap, axis=0, keepdims=True)
+
+        plane[4, place, 12:13] = lax.fori_loop(0, 8, step, jnp.zeros((1, 256), F32), unroll=2)
+        plane[4, place, 13:] = jnp.zeros((3, 256), F32)
+
+    def relay_last():
+        @pl.when(c == 1)
+        def _():
+            def end(e, carry):
+                plane_copy(4, 16, e).wait_recv()
+                return carry
+
+            lax.fori_loop(1, 16, end, 0)
+            sums = jnp.sum(plane[4], axis=0)
+            step = vectors[4] - vectors[5]
+            gaps, masks_ = sums[:8], counts[...]
+            square = jnp.sum((2.0 * gaps + masks_ * step) * step, axis=0, keepdims=True)
+            row = lax.broadcasted_iota(jnp.int32, (8, 256), 0)
+            tail_ = sums[8:] + jnp.where(row == 4, square, 0.0)
+            start_line(4, jnp.concatenate([gaps + masks_ * step, tail_], axis=0))
 
     def settle(total, prices, norms, k):
         mean = total * (1.0 / AGENTS)
@@ -388,14 +439,15 @@
     v, shared, prices, norms = settle(end_line(2, 8) + end_line(6, 8), prices, norms, 3)
     advance(4, v, ex=7)
     relay(3, 8)
-    v, shared, prices, norms = settle(end_line(3, 8) + end_line(7, 8), prices, norms, 4)
+    foreseen()
+    start_plane(4, 16)
+    usage_sum = end_line(3, 8) + end_line(7, 8)
+    v, shared, prices, norms = settle(usage_sum, prices, norms, 4)
     advance(5, v)
     for e in (1, 7, 2):
         back_copy(e).start()
-    plane[4, place, 13:] = jnp.zeros((3, 256), F32)
-    start_plane(4, 16)
     back[kind] = usage[z, pl.ds(pl.multiple_of(c * 64, 64), 64)]
-    relay(4, 16)
+    relay_last()
     for e in (1, 7, 2):
         back_copy(e).wait_recv()
     result = jnp.zeros((256, 256), F32)
@@ -407,7 +459,7 @@
     usage_store = pltpu.make_async_copy(usage_out, usage_hbm, out_store)
     usage_store.start()
     total = end_line(4, 16)
-    v, shared, prices, norms = settle(total[:8], prices, norms, 5)
+    v, shared, prices, norms = settle(usage_sum + total[:8], prices, norms, 5)
     duals = jnp.zeros((1, 128), F32)
     for k in range(ITERS):
         duals = jnp.where(norm_lane == k, jnp.sum(total[8 + k : 9 + k]), duals)
@@ -435,11 +487,8 @@
         hand_copy(d).wait_send()
     for d in range(1, 8):
         row_copy(d).wait_send()
-        z_copy(d).wait_send()
-        for s in (1, 2, 3):
-            one_copy(d, s).wait_send()
-            two_copy(d, s).wait_send()
-        core_copy(d).wait_send()
+        sized(z, lambda width: z_copy(d, width).wait_send())
+        sized(source(d), functools.partial(end_parts, d))
     for e in (1, 7, 2):
         back_copy(e).wait_send()
 
@@ -479,7 +528,7 @@
             pltpu.VMEM((144, 2048), BF16),
             pltpu.VMEM((128, 2048), BF16),
             pltpu.VMEM((8, 256), F32),
-            pltpu.VMEM((5, 8, 256), F32),
+            pltpu.VMEM((6, 8, 256), F32),
             pltpu.VMEM((ITERS, 16, 16, 256), F32),
             pltpu.VMEM((8, 4, 16, 256), F32),
             pltpu.VMEM((4, 64, 256), F32),

time: 80.8 us -> 78.5 us (0.972); the launches traced: 79.6 us -> 78.4 us
  Pallas kernels: 78.9 us -> 77.7 us
    pallas_call x1, Pallas kernels: 77.3 us -> 76 us  [on_device(): pl.pallas_call(kernel, out_shape=(jax.ShapeDtypeStruct((256, 256), F32),...]
where the time goes in v6:
time: 78.5 us; the launch traced here: 78.4 us
  Pallas kernels  77.7 us (99%)
    pallas_call x1, Pallas kernels, on_device(): pl.pallas_call(kernel, out_shape=(jax.ShapeDtypeStruct((256, 256), F32),...  76 us
    pallas_call x1, Pallas kernels, on_device(): pl.pallas_call(hand_over, out_shape=(jax.ShapeDtypeStruct((256, 256), F32...  1.68 us

profile of v6, /device:TPU:32, one launch (start us, length us, event | category | flops | bytes accessed | tf_op | source)
XLA Modules:
  0.0 78.4 jit_solution(12708126104953318813)
XLA Ops:
  0.6 76.0 %admm.1 = (f32[256,256]{1,0:T(8,128)}, f32[4,256]{1,0:T(4,128)}) custom-call(f32[256,256]{1,0:T(8,128)} %cost_hbm.1, s32[1,256]{1,0:T(1,128)} %bitcast.11, s32[2,256]{1,0:T(2,128)} %bitcast.10, f32[1,256]{1,0:T(1,128)} %bitcast.12, f32[1,256]{1,0:T(1,128)} %bitcast.13, bf16[4,4,4,16,2048]{4,3,2,1,0:T(8,128)(2,1)} %bitcast.9), custom_call_target="tpu_custom_call" | custom-call | tf_op jit(solution)/shard_map/admm/pallas_call | solution.py:508
  76.7 1.7 %hand_over.1 = (f32[256,256]{1,0:T(8,128)}, f32[1,256]{1,0:T(1,128)}, f32[1,256]{1,0:T(1,128)}, f32[1,5]{1,0:T(1,128)}, f32[1,5]{1,0:T(1,128)}) custom-call(f32[256,256]{1,0:T(8,128)} %get-tuple-element.12.usage_ref, f32[4,256]{1,0:T(4,128)} %get-tuple-element.13.small_ref), custom_call_target="tpu_custom_call" | custom-call | tf_op jit(solution)/shard_map/hand_over/pallas_call | solution.py:558

commit v7 on v6

--- a/solution.py
+++ b/solution.py
@@ -146,7 +146,7 @@
     for t in range(4):
         packed[t, :64] = cost[t * 64 : (t + 1) * 64]
         turned = masks if t == 0 else pltpu.roll(masks, 256 - 64 * t, 1)
-        packed[t, 64:] = jnp.where((line < 2) & (lane < 64), turned, tail).astype(BF16)
+        packed[t, 64:] = jnp.where((line < 2) & (lane < 64), turned, tail)[:8].astype(BF16)
 
     def row_copy(d):
         far = (z + d) % 8
@@ -251,7 +251,7 @@
             vectors[1, j : j + 1] = ends[5:6] + ends[6:7] + ends[7:8]
             for side in range(2):
                 here = rows[j, side, 64:, :128]
-                spread = lax.dot_general(here, wide, (((0,), (0,)), ((), ())), preferred_element_type=F32)
+                spread = lax.dot_general(here, wide[:8], (((0,), (0,)), ((), ())), preferred_element_type=F32)
                 expand[j, side * 64 : side * 64 + 64] = spread[:64]
         usage[...] = jnp.zeros((8, 128, 256), F32)
         fill(z)
@@ -348,7 +348,7 @@
             place_columns(k, j, opened(j) * expand[j])
             return carry
 
-        lax.fori_loop(0, 8, step, 0, unroll=2)
+        lax.fori_loop(0, 8, step, 0, unroll=8)
 
     def advance(k, v, ex=None):
         vectors[4] = v
@@ -368,7 +368,7 @@
                 plain[:, lanes_of(j)] = (fresh - costs_of(j)).astype(BF16)
             return change + jnp.sum(gap * gap, axis=0, keepdims=True)
 
-        change = lax.fori_loop(0, 8, step, jnp.zeros((1, 256), F32), unroll=2)
+        change = lax.fori_loop(0, 8, step, jnp.zeros((1, 256), F32), unroll=8)
         if ex is not None:
             plane[4, place, 7 + k : 8 + k] = change
 
@@ -384,7 +384,7 @@
             place_columns(4, j, gap)
             return change + jnp.sum(gap * gap, axis=0, keepdims=True)
 
-        plane[4, place, 12:13] = lax.fori_loop(0, 8, step, jnp.zeros((1, 256), F32), unroll=2)
+        plane[4, place, 12:13] = lax.fori_loop(0, 8, step, jnp.zeros((1, 256), F32), unroll=8)
         plane[4, place, 13:] = jnp.zeros((3, 256), F32)
 
     def relay_last():
@@ -418,7 +418,7 @@
         place_columns(0, j, fresh)
         return change + jnp.sum(fresh * fresh, axis=0, keepdims=True)
 
-    plane[4, place, 8:9] = lax.fori_loop(0, 8, opening, jnp.zeros((1, 256), F32), unroll=2)
+    plane[4, place, 8:9] = lax.fori_loop(0, 8, opening, jnp.zeros((1, 256), F32), unroll=8)
     start_plane(0, 8)
     for j in range(8):
         plane[1, place, 8 + j : 9 + j] = jnp.sum(expand[j], axis=0, keepdims=True)
@@ -521,8 +521,8 @@
             pltpu.VMEM((2, 8, 4, 4, 16, 640), BF16),
             pltpu.VMEM((8, 2048, 256), BF16),
             pltpu.VMEM((256, 256), BF16),
-            pltpu.VMEM((4, 80, 256), BF16),
-            pltpu.VMEM((8, 2, 80, 256), BF16),
+            pltpu.VMEM((4, 72, 256), BF16),
+            pltpu.VMEM((8, 2, 72, 256), BF16),
             pltpu.VMEM((8, 128, 256), F32),
             pltpu.VMEM((8, 128, 256), F32),
             pltpu.VMEM((144, 2048), BF16),

time: 78.5 us -> 74.5 us (0.949)
  Pallas kernels: 77.7 us -> 73.7 us
    pallas_call x1, Pallas kernels: 76 us -> 72 us  [on_device(): pl.pallas_call(kernel, out_shape=(jax.ShapeDtypeStruct((256, 256), F32),...]
where the time goes in v7:
time: 74.5 us; the launch traced here: 74.4 us
  Pallas kernels  73.7 us (99%)
    pallas_call x1, Pallas kernels, on_device(): pl.pallas_call(kernel, out_shape=(jax.ShapeDtypeStruct((256, 256), F32),...  72 us
    pallas_call x1, Pallas kernels, on_device(): pl.pallas_call(hand_over, out_shape=(jax.ShapeDtypeStruct((256, 256), F32...  1.68 us

profile of v7, /device:TPU:32, one launch (start us, length us, event | category | flops | bytes accessed | tf_op | source)
XLA Modules:
  0.0 74.4 jit_solution(18138970032140057746)
XLA Ops:
  0.6 72.0 %admm.1 = (f32[256,256]{1,0:T(8,128)}, f32[4,256]{1,0:T(4,128)}) custom-call(f32[256,256]{1,0:T(8,128)} %cost_hbm.1, s32[1,256]{1,0:T(1,128)} %bitcast.11, s32[2,256]{1,0:T(2,128)} %bitcast.10, f32[1,256]{1,0:T(1,128)} %bitcast.12, f32[1,256]{1,0:T(1,128)} %bitcast.13, bf16[4,4,4,16,2048]{4,3,2,1,0:T(8,128)(2,1)} %bitcast.9), custom_call_target="tpu_custom_call" | custom-call | tf_op jit(solution)/shard_map/admm/pallas_call | solution.py:508
  72.7 1.7 %hand_over.1 = (f32[256,256]{1,0:T(8,128)}, f32[1,256]{1,0:T(1,128)}, f32[1,256]{1,0:T(1,128)}, f32[1,5]{1,0:T(1,128)}, f32[1,5]{1,0:T(1,128)}) custom-call(f32[256,256]{1,0:T(8,128)} %get-tuple-element.12.usage_ref, f32[4,256]{1,0:T(4,128)} %get-tuple-element.13.small_ref), custom_call_target="tpu_custom_call" | custom-call | tf_op jit(solution)/shard_map/hand_over/pallas_call | solution.py:558
